TPU v7x, 512 devices: a 4x2x32 block of a 4x8x32 slice. The times are simulated.
512 devices in a mesh: groups: 2 (over y), blk: 32 (over z), head: 4 (over x), pair: 2 (over core).
Axes of the slice: x: 4, y: 2, z: 32, core: 2. Of those that a mesh axis runs over, the one named last changes fastest.
The devices are a block of a 4x8x32 slice.
Arguments:
- single: bfloat16 [2048, 384], P(('groups', 'blk')), parts along dimension 0, may hold values from -6 to 6
- pair: bfloat16 [2048, 32, 32, 128], P(('groups', 'blk'), None, 'pair'), parts along dimension 0, may hold values from -6 to 6
- frames: float32 [12, 2048], P(None, ('groups', 'blk')), parts along dimension 1, as said below
- chain: int32 [2048], P(('groups', 'blk')), parts along dimension 0, may hold values from 0 to 5, never falling along the last dimension, each value on 1 to 341 neighbouring positions
- mask: int32 [2048], P(('groups', 'blk')), parts along dimension 0, may hold values 0 or 1
- w_query: bfloat16 [384, 192], P(None, 'head'), may hold values from -0.3125 to 0.3125
- w_key_value: bfloat16 [384, 384], P(None, 'head'), may hold values from -0.3125 to 0.3125
- w_query_points: bfloat16 [384, 144], P(None, 'head'), may hold values from -0.3125 to 0.3125
- w_kv_points: bfloat16 [384, 432], P(None, 'head'), may hold values from -0.3125 to 0.3125
- w_pair_bias: bfloat16 [128, 12], P(None, 'head'), may hold values from -0.5 to 0.5
- head_weights: float32 [12], P('head'), may hold values from -9 to 1
- chain_bias: float32 [12], P('head'), may hold values from -3 to 3
- w_out: bfloat16 [12, 176, 384], P('head'), may hold values from -0.125 to 0.125
- out_gain: float32 [384], replicated, may hold values from 0.5 to 1.5
- w_backbone: bfloat16 [384, 6], replicated, may hold values from -0.3125 to 0.3125
Outputs:
- single_out: bfloat16 [2048, 384], P(('groups', 'blk')), parts along dimension 0
- frames_out: float32 [12, 2048], P(None, 'groups'), parts along dimension 1
There are 2 independent parts, one for each index of `groups`. A program takes and returns all parts, laid end to end along the dimension named above; an argument that names none is the same for every part. Nothing has to cross between parts.
Inputs may be any that keep to these rules, and one draw needn't show every extreme that they name: `frames`: rows 0 to 8 of every column hold an orthonormal rotation matrix row by row; rows 9 to 11 the translation.
All inputs are finite; a program needn't handle non-finite values. No bound on the sum of `mask` on one device may be relied on, other than what follows from the above.
Results may differ from a plain program's by a relative error of at most 0.0048.
Values sent between devices are 32-bit elements; how exact they have to be, the bound alone decides.
No kernel may reach another device: no remote copies, remote signals or barrier semaphores. Data moves between devices by JAX's collectives and lax.ppermute only.
A program may use at most 64 MiB of HBM per device.

v0:
```python
import math

import jax
import jax.numpy as jnp
from jax import lax
from jax.sharding import PartitionSpec as P

HIGH = lax.Precision.HIGHEST
LOGIT_WEIGHT = math.sqrt(1.0 / 3.0)
MASK_PENALTY = 100000.0


def side_by_side(arrays, axis, dim, along):
    widths = [a.shape[along] for a in arrays]
    both = jnp.concatenate(arrays, axis=along)
    out = lax.all_gather(both, axis, axis=dim, tiled=True)
    return tuple(jnp.split(out, [sum(widths[:k]) for k in range(1, len(widths))], axis=along))


def copy_for_each(array, axis):
    copies = jnp.broadcast_to(array, (lax.axis_size(axis), *array.shape))
    return lax.all_to_all(copies, axis, split_axis=0, concat_axis=0, tiled=True)


def all_in_one(array, axis):
    leaves = jax.tree.leaves(array)
    order = sorted(range(len(leaves)), key=lambda k: -leaves[k].size)
    width = (1, *leaves[order[0]].shape)[-1]
    lines = [
        jnp.pad(leaves[k].reshape(-1), (0, -leaves[k].size % width)).reshape(-1, width)
        for k in order
    ]
    both, at, found = (copy_for_each(jnp.concatenate(lines), axis), 0, {})
    for k, line in zip(order, lines):
        section = both[:, at : at + len(line)].reshape(len(both), -1)
        found[k] = section[:, : leaves[k].size].reshape(-1, *leaves[k].shape)
        at += len(line)
    numbers = iter(range(len(leaves)))
    return jax.tree.map(lambda _: found[next(numbers)], array)


def joined_by_halves(pieces, combine):
    while len(jax.tree.leaves(pieces)[0]) > 1:
        pieces = jax.vmap(combine)(
            *(jax.tree.map(lambda part: part[side::2], pieces) for side in (0, 1))
        )
    return jax.tree.map(lambda part: part[0], pieces)


def merged_2(array, axis, combine):
    pieces = all_in_one(array, axis)
    return joined_by_halves(pieces, combine)


def over_copies(array, axis):
    return copy_for_each(array, axis).sum(axis=0)


def laid_out(blocks, dim):
    dims = list(blocks.shape[1:])
    dims[dim] *= blocks.shape[0]
    return jnp.moveaxis(blocks, 0, dim).reshape(dims)


def collect(array, axis, dim):
    blocks = copy_for_each(array, axis)
    return laid_out(blocks, dim)


def to_global(local, frames):
    rotation = frames[:9].reshape(3, 3, -1)
    moved = jnp.einsum("abn,ngb->nga", rotation, local, precision=HIGH)
    return moved + jnp.transpose(frames[9:12])[:, None, :]


def to_local(points, frames):
    rotation = frames[:9].reshape(3, 3, -1)
    moved = points - jnp.transpose(frames[9:12])[:, None, None, :]
    return jnp.einsum("abn,nhpa->nhpb", rotation, moved, precision=HIGH)


def compose(frames, motion):
    rotation = frames[:9].reshape(3, 3, -1)
    inverse = 1.0 / jnp.sqrt(1.0 + motion[:, 0] ** 2 + motion[:, 1] ** 2 + motion[:, 2] ** 2)
    quat_b = motion[:, 0] * inverse
    quat_c = motion[:, 1] * inverse
    quat_d = motion[:, 2] * inverse
    spin = jnp.stack(
        [
            inverse * inverse + quat_b * quat_b - quat_c * quat_c - quat_d * quat_d,
            2.0 * (quat_b * quat_c - inverse * quat_d),
            2.0 * (quat_b * quat_d + inverse * quat_c),
            2.0 * (quat_b * quat_c + inverse * quat_d),
            inverse * inverse - quat_b * quat_b + quat_c * quat_c - quat_d * quat_d,
            2.0 * (quat_c * quat_d - inverse * quat_b),
            2.0 * (quat_b * quat_d - inverse * quat_c),
            2.0 * (quat_c * quat_d + inverse * quat_b),
            inverse * inverse - quat_b * quat_b - quat_c * quat_c + quat_d * quat_d,
        ]
    ).reshape(3, 3, -1)
    new_rotation = jnp.einsum("abn,bcn->acn", rotation, spin, precision=HIGH)
    offset = jnp.einsum("abn,nb->an", rotation, motion[:, 3:6], precision=HIGH)
    return jnp.concatenate([new_rotation.reshape(9, -1), frames[9:12] + offset], axis=0)


def attention_logits(
    pair_rows,
    query_rows,
    query_points,
    query_chain,
    query_present,
    keys,
    key_points,
    key_chain,
    key_present,
    w_pair_bias,
    distance_scale,
    chain_bias,
):
    count_q = pair_rows.shape[0]
    count_k = pair_rows.shape[1]
    bias = jnp.dot(
        pair_rows.reshape(count_q * count_k, -1), w_pair_bias, preferred_element_type=jnp.float32
    ).reshape(count_q, count_k, -1)
    dots = jnp.einsum("ihc,jhc->ijh", query_rows, keys, precision=HIGH) / math.sqrt(keys.shape[-1])
    gaps = query_points[:, None] - key_points[None]
    distance = jnp.sum(gaps * gaps, axis=(3, 4))
    differ = (query_chain[:, None] != key_chain[None, :]).astype(jnp.float32)
    logits = LOGIT_WEIGHT * (
        dots + bias - distance_scale * distance + chain_bias * differ[..., None]
    )
    absent = 1.0 - query_present[:, None] * key_present[None, :]
    return logits - MASK_PENALTY * absent[..., None]


def rescale(values, factor):
    return values * factor.reshape(factor.shape + (1,) * (values.ndim - factor.ndim))


def fold_pair(first, second):
    best = jnp.maximum(first[0], second[0])
    first_scale = jnp.exp(first[0] - best)
    second_scale = jnp.exp(second[0] - best)
    merged = [
        rescale(left_part, first_scale) + rescale(right_part, second_scale)
        for left_part, right_part in zip(first[1:], second[1:])
    ]
    return (best,) + tuple(merged)


def body(
    single,
    pair,
    frames,
    chain,
    mask,
    w_query,
    w_key_value,
    w_query_points,
    w_kv_points,
    w_pair_bias,
    head_weights,
    chain_bias,
    w_out,
    out_gain,
    w_backbone,
):
    rows = single.shape[0]
    half = pair.shape[2]
    width = pair.shape[3]
    heads_here = w_pair_bias.shape[1]
    head_size = w_query.shape[1] // heads_here
    query_count = w_query_points.shape[1] // (3 * heads_here)
    value_count = w_kv_points.shape[1] // (3 * heads_here) - query_count
    pair_keys = pair.reshape(rows, pair.shape[1] * half, width)
    query = jnp.dot(single, w_query, preferred_element_type=jnp.float32).reshape(
        rows, heads_here, head_size
    )
    query_local = jnp.dot(single, w_query_points, preferred_element_type=jnp.float32)
    query_points = to_global(query_local.reshape(rows, heads_here * query_count, 3), frames)
    query_points = query_points.reshape(rows, heads_here, query_count, 3)
    query_chain = chain.astype(jnp.float32)
    query_present = mask.astype(jnp.float32)
    distance_scale = jax.nn.softplus(head_weights) * math.sqrt(2.0 / (9.0 * query_count)) / 2.0
    position = lax.axis_index("pair")
    key_single = lax.dynamic_slice_in_dim(single, position * half, half, 0)
    key_frames = lax.dynamic_slice_in_dim(frames, position * half, half, 1)
    key_chain = lax.dynamic_slice_in_dim(query_chain, position * half, half, 0)
    key_present = lax.dynamic_slice_in_dim(query_present, position * half, half, 0)
    key_value = jnp.dot(key_single, w_key_value, preferred_element_type=jnp.float32)
    key_local = jnp.dot(key_single, w_kv_points, preferred_element_type=jnp.float32)
    key_global = to_global(
        key_local.reshape(half, heads_here * (query_count + value_count), 3), key_frames
    )
    payload = jnp.concatenate([key_value, key_global.reshape(half, -1)], axis=1)
    key_meta = jnp.stack([key_chain, key_present], axis=1)
    split_at = heads_here * 2 * head_size
    pieces = side_by_side((payload, key_meta), "blk", 0, 1)
    moving = pieces[0]
    moving_meta = pieces[1]
    top = jnp.full((rows, heads_here), -1e30, jnp.float32)
    count = moving.shape[0]
    absorb_pieces = moving[:, :split_at].reshape(count, heads_here, 2, head_size)
    points = moving[:, split_at:].reshape(count, heads_here, query_count + value_count, 3)
    logits = attention_logits(
        pair_keys,
        query,
        query_points,
        query_chain,
        query_present,
        absorb_pieces[:, :, 0],
        points[:, :, :query_count],
        moving_meta[:, 0],
        moving_meta[:, 1],
        w_pair_bias,
        distance_scale,
        chain_bias,
    )
    new_top = jnp.maximum(top, jnp.max(logits, axis=1))
    weights = jnp.exp(logits - new_top[:, None, :])
    total = jnp.sum(weights, axis=1)
    sum_values = jnp.einsum("ijh,jhc->ihc", weights, absorb_pieces[:, :, 1], precision=HIGH)
    sum_points = jnp.einsum("ijh,jhpd->ihpd", weights, points[:, :, query_count:], precision=HIGH)
    sum_pair = jnp.einsum(
        "ijh,ijc->ihc", weights.astype(jnp.bfloat16), pair_keys, preferred_element_type=jnp.float32
    )
    carry = (new_top, total, sum_values, sum_points, sum_pair)
    best, total, sum_values, sum_points, sum_pair = merged_2(carry, "pair", fold_pair)
    attended = sum_values / total[..., None]
    pointed = to_local(sum_points / total[..., None, None], frames)
    point_norms = jnp.sqrt(jnp.sum(pointed * pointed, axis=3) + 1.0)
    paired = sum_pair / total[..., None]
    joined = jnp.concatenate(
        [attended, pointed.reshape(rows, heads_here, value_count * 3), point_norms, paired], axis=2
    ).astype(jnp.bfloat16)
    partial_update = jnp.dot(
        joined.reshape(rows, -1),
        w_out.reshape(-1, w_out.shape[2]),
        preferred_element_type=jnp.float32,
    )
    update = over_copies(partial_update, "head")
    mixed = single.astype(jnp.float32) + update
    centre = jnp.mean(mixed, axis=1, keepdims=True)
    spread = jnp.mean(jnp.square(mixed - centre), axis=1, keepdims=True)
    single_out = ((mixed - centre) * lax.rsqrt(spread + 1e-05) * out_gain).astype(jnp.bfloat16)
    motion = jnp.dot(single_out, w_backbone, preferred_element_type=jnp.float32)
    frames_new = compose(frames, motion)
    frames_out = collect(frames_new, "blk", 1)
    return (single_out, frames_out)


def solution(mesh):
    placed = (
        P(("groups", "blk"), None),
        P(("groups", "blk"), None, "pair", None),
        P(None, ("groups", "blk")),
        P(("groups", "blk")),
        P(("groups", "blk")),
        P(None, "head"),
        P(None, "head"),
        P(None, "head"),
        P(None, "head"),
        P(None, "head"),
        P("head"),
        P("head"),
        P("head", None, None),
        P(),
        P(),
    )
    return jax.shard_map(
        body,
        mesh=mesh,
        in_specs=placed,
        out_specs=(P(("groups", "blk"), None), P(None, "groups")),
        check_vma=False,
    )
```

profile of v0, /device:TPU:40, one launch (start us, length us, event | category | flops | bytes accessed | tf_op | source)
XLA Modules:
  0.0 169.9 jit_solution(1981582161542075526)
XLA Ops:
  0.7 0.8 slice_bitcast_fusion.4
  1.5 0.8 constant_dynamic-slice_fusion
  2.3 1.1 fusion.40
  3.6 0.8 dynamic-slice_bitcast_fusion
  4.4 0.2 convolution_add_fusion.1
  4.7 0.1 copy.224
  4.9 0.7 convert_element_type.27
  5.6 0.7 convert_element_type.28
  6.5 1.0 fusion.42
  7.6 97.4 %all_gather.3 = f32[512,206]{1,0:T(8,128)S(1)} all-gather(f32[16,206]{1,0:T(8,128)S(1)} %pad_maximum_fusion), channel_id=1, replica_groups=mesh['groups'=2,'blk'=32,'head'=4,'pair'=2] {'blk'}, dimensions={0}, use_global_device_ids=true | all-gather | bytes 435072 | tf_op jit(solution)/shard_map/all_gather | solution.py:16
  105.0 0.1 slice.190
  105.1 0.4 slice_reduce_fusion.1
  105.5 0.1 copy.238
  105.9 0.1 copy.234
  106.1 0.1 fusion.64
  106.2 0.1 copy.233
  106.4 0.3 convolution_add_fusion
  107.0 0.1 copy.281
  107.1 0.1 fusion.63
  107.3 0.3 multiply_reduce_fusion
  107.6 3.4 %fusion.44 = f32[32,512,3]{1,2,0:T(4,128)S(1)} fusion(bf16[32,512,128]{2,1,0:T(8,128)(2,1)} %bitcast.174, bf16[128,3]{0,1:T(4,128)(2,1)S(1)} %copy-done.8), kind=kOutput, calls=%fused_computation.78 | convolution fusion | flops 12582912 | bytes 4391680 | tf_op jit(solution)/shard_map/dot_general | solution.py:122
  111.0 0.5 fusion.62
  111.5 0.4 convolution_bitcast_fusion.3
  111.9 0.2 fusion.20
  112.3 0.4 convolution_bitcast_fusion.2
  112.7 0.2 copy.241
  113.0 0.2 reshape.658
  113.2 2.8 %fusion.18 = f32[32,3,128]{2,1,0:T(4,128)S(1)} fusion(bf16[32,512,128]{2,1,0:T(8,128)(2,1)} %bitcast.175, bf16[32,512,3]{1,0,2:T(8,128)(2,1)S(1)} %get-tuple-element.14), kind=kOutput, calls=%fused_computation.30 | convolution fusion | flops 12582912 | bytes 4341760 | tf_op jit(solution)/shard_map/ijh,ijc->ihc/dot_general | solution.py:224
  116.4 0.1 concatenate.14
  116.6 3.9 %all_to_all.15 = f32[2,128,128]{2,1,0:T(8,128)S(1)} all-to-all(f32[2,128,128]{2,1,0:T(8,128)S(1)} %broadcast_in_dim.9), channel_id=1, replica_groups=mesh['groups'=2,'blk'=32,'head'=4,'pair'=2] {'pair'}, dimensions={0} | all-to-all | bytes 262144 | tf_op jit(solution)/shard_map/all_to_all | solution.py:22
  121.2 0.1 slice.163
  121.4 0.3 slice.177
  121.7 0.3 slice.179
  122.0 0.1 copy.272
  122.1 3.9 %fusion.57 = (bf16[32,3,8,3]{2,3,1,0:T(4,128)(2,1)S(1)}, f32[32,3,8]{2,1,0:T(4,128)S(1)}) fusion(f32[3,3,32,1]{0,1,3,2:T(4,128)S(1)} %copy.272, f32[32,3,8,3]{3,2,1,0:T(8,128)S(1)} %slice.179, f32[32,3,8,3]{3,2,1,0:T(8,128)S(1)} %slice.177, f32[32,3]{1,0:T(8,128)S(1)} %copy.235, f32[32,3]{1,0:T(8,128)S(1)} %get-tuple-element.10, ...), kind=kOutput, calls=%fused_computation.116 | convolution fusion | flops 100608 | bytes 28800 | tf_op jit(solution)/shard_map/abn,nhpa->nhpb/dot_general | solution.py:79
  126.0 0.1 copy.254
  126.7 0.3 convolution_bitcast_fusion.1
  127.1 10.7 %all_to_all.16 = f32[4,32,384]{2,1,0:T(8,128)S(1)} all-to-all(f32[4,32,384]{2,1,0:T(8,128)S(1)} %broadcast_in_dim.10), channel_id=1, replica_groups=mesh['groups'=2,'blk'=32,'head'=4,'pair'=2] {'head'}, dimensions={0} | all-to-all | bytes 393216 | tf_op jit(solution)/shard_map/all_to_all | solution.py:22
  137.8 0.1 fusion.37
  137.9 0.2 multiply_reduce_fusion.2
  138.2 0.1 fusion.65
  138.5 0.1 copy.263
  138.6 0.3 convolution_bitcast_fusion
  139.1 0.1 reshape.699
  139.3 28.4 %all_to_all.17 = f32[32,1,384]{2,1,0:T(1,128)S(1)} all-to-all(f32[32,1,384]{2,1,0:T(1,128)S(1)} %reshape.699), channel_id=1, replica_groups=mesh['groups'=2,'blk'=32,'head'=4,'pair'=2] {'blk'}, dimensions={0} | all-to-all | bytes 98304 | tf_op jit(solution)/shard_map/all_to_all | solution.py:22
  167.7 0.5 broadcast.233
  168.2 0.8 reduce.22
  169.2 0.8 reshape.668
  (98 shorter events, 3.9 us)
Async XLA Ops:
  0.6 126.1 %copy-start = (bf16[3,176,384]{2,1,0:T(8,128)(2,1)S(1)}, bf16[3,176,384]{2,1,0:T(8,128)(2,1)}, u32[]{:S(2)}) copy-start(bf16[3,176,384]{2,1,0:T(8,128)(2,1)} %param.27) | copy-start | bytes 1216516
  0.6 105.2 %copy-start.3 = (f32[12,32]{1,0:T(8,128)S(1)}, f32[12,32]{1,0:T(8,128)}, u32[]{:S(2)}) copy-start(f32[12,32]{1,0:T(8,128)} %param.17) | copy-start | bytes 4612
  0.7 105.4 %copy-start.1 = (bf16[32,384]{1,0:T(8,128)(2,1)S(1)}, bf16[32,384]{1,0:T(8,128)(2,1)}, u32[]{:S(2)}) copy-start(bf16[32,384]{1,0:T(8,128)(2,1)} %param.15) | copy-start | bytes 73732
  0.7 105.4 %copy-start.5 = (bf16[384,36]{0,1:T(8,128)(2,1)S(1)}, bf16[384,36]{0,1:T(8,128)(2,1)}, u32[]{:S(2)}) copy-start(bf16[384,36]{0,1:T(8,128)(2,1)} %param.22) | copy-start | bytes 82948
  0.7 106.4 %copy-start.4 = (bf16[384,48]{0,1:T(8,128)(2,1)S(1)}, bf16[384,48]{0,1:T(8,128)(2,1)}, u32[]{:S(2)}) copy-start(bf16[384,48]{0,1:T(8,128)(2,1)} %param.20) | copy-start | bytes 110596
  0.7 106.5 %copy-start.10 = (f32[3]{0:T(128)S(1)}, f32[3]{0:T(128)}, u32[]{:S(2)}) copy-start(f32[3]{0:T(128)} %param.25) | copy-start | bytes 40
  0.7 106.9 %copy-start.8 = (bf16[128,3]{0,1:T(4,128)(2,1)S(1)}, bf16[128,3]{0,1:T(4,128)(2,1)}, u32[]{:S(2)}) copy-start(bf16[128,3]{0,1:T(4,128)(2,1)} %param.24) | copy-start | bytes 2308
  105.5 5.5 %copy-start.9 = (f32[3]{0:T(128)S(1)}, f32[3]{0:T(128)}, u32[]{:S(2)}) copy-start(f32[3]{0:T(128)} %param.26) | copy-start | bytes 40
  116.0 22.1 %copy-start.7 = (f32[384]{0:T(512)S(1)}, f32[384]{0:T(512)}, u32[]{:S(2)}) copy-start(f32[384]{0:T(512)} %param.28) | copy-start | bytes 4612
  116.1 22.1 %copy-start.6 = (bf16[384,6]{0,1:T(8,128)(2,1)S(1)}, bf16[384,6]{0,1:T(8,128)(2,1)}, u32[]{:S(2)}) copy-start(bf16[384,6]{0,1:T(8,128)(2,1)} %param.29) | copy-start | bytes 13828
  138.2 31.7 %copy-start.2 = (bf16[32,384]{1,0:T(8,128)(2,1)}, bf16[32,384]{1,0:T(8,128)(2,1)S(1)}, u32[]{:S(2)}) copy-start(bf16[32,384]{1,0:T(8,128)(2,1)S(1)} %multiply_convert_fusion) | copy-start | bytes 73732
where the time goes:
time: 170 us
  blocking collectives  140 us (82%)
  matrix products  15 us (9%)
  local copies, waits for them, and re-layouts  9.68 us (6%)
  other arithmetic  3.57 us (2%)
    all_gather x1, blocking collectives, side_by_side(): out = lax.all_gather(both, axis, axis=dim, tiled=True)  97.4 us
    all_to_all x3, blocking collectives, copy_for_each(): return lax.all_to_all(copies, axis, split_axis=0, concat_axis=0, tiled=True)  43 us
    dot_general x1, matrix products, to_local(): return jnp.einsum('abn,nhpa->nhpb', rotation, moved, precision=HIGH)  3.88 us

commit v1 on v0

v1 whole, which is shorter than its diff:
```python
import functools
import math

import jax
import jax.numpy as jnp
from jax import lax
from jax.experimental import pallas as pl
from jax.experimental.pallas import tpu as pltpu
from jax.sharding import Mesh
from jax.sharding import PartitionSpec as P

HIGH = lax.Precision.HIGHEST
LOGIT_WEIGHT = math.sqrt(1.0 / 3.0)
MASK_PENALTY = 100000.0
F32 = jnp.float32
BF16 = jnp.bfloat16

SLOTS = 4
HALF = 128
COMP = 40
CHAIN, PRESENT, ONE, TOP = 120, 121, 122, 123
VMEM = pl.BlockSpec(memory_space=pltpu.VMEM)
SMEM = pl.BlockSpec(memory_space=pltpu.SMEM)


def iota(shape, dim):
    return lax.broadcasted_iota(jnp.int32, shape, dim)


def dot(a, b, precision=None):
    return jnp.dot(a, b, preferred_element_type=F32, precision=precision)


def rotated(frames_ref, parts):
    moved = []
    for a in range(3):
        total = frames_ref[3 * a : 3 * a + 1, :] * parts[0]
        for b in (1, 2):
            total += frames_ref[3 * a + b : 3 * a + b + 1, :] * parts[b]
        moved.append(total + frames_ref[9 + a : 10 + a, :])
    return moved


def project_kernel(
    heads,
    size,
    n_query,
    n_points,
    single_ref,
    frames_ref,
    chain_ref,
    mask_ref,
    wq_ref,
    wkv_ref,
    wqp_ref,
    wkp_ref,
    hw_ref,
    cb_ref,
    payload_ref,
    qb_ref,
    qaux_ref,
    frows_ref,
    flat,
    turned,
    points,
    full,
    spread,
):
    rows = single_ref.shape[0]
    half = payload_ref.shape[0]
    x = single_ref[...]
    q_wide = heads * size
    flat[...] = jnp.zeros_like(flat)
    flat[:, 0:q_wide] = dot(x, wq_ref[...])
    flat[:, HALF : HALF + 3 * heads * n_query] = dot(x, wqp_ref[...])
    flat[:, 2 * HALF : 2 * HALF + 3 * heads * n_points] = dot(x, wkp_ref[...])
    full[...] = jnp.zeros_like(full)
    full[:, 0 : 2 * q_wide] = dot(x, wkv_ref[...])
    for k in range(3):
        turned[k * HALF : (k + 1) * HALF, :] = flat[:, k * HALF : (k + 1) * HALF].T
    chain_row = chain_ref[...].astype(F32).reshape(1, rows)
    mask_row = mask_ref[...].astype(F32).reshape(1, rows)

    count = heads * n_points
    local = [turned[pl.ds(2 * HALF + b, count, stride=3), :] for b in range(3)]
    points[...] = jnp.zeros_like(points)
    for a, value in enumerate(rotated(frames_ref, local)):
        points[COMP * a : COMP * a + count, :] = value
    points[CHAIN : CHAIN + 1, :] = chain_row
    points[PRESENT : PRESENT + 1, :] = mask_row
    points[ONE : ONE + 1, :] = jnp.ones((1, rows), F32)
    full[:, HALF:] = points[...].T
    start = pl.multiple_of(lax.axis_index("pair") * half, half)
    payload_ref[...] = full[pl.ds(start, half), :]

    count = heads * n_query
    local = [turned[pl.ds(HALF + b, count, stride=3), :] for b in range(3)]
    spread[...] = jnp.zeros_like(spread)
    spread[0:q_wide, :] = turned[0:q_wide, :]
    for a, value in enumerate(rotated(frames_ref, local)):
        spread[48 + 16 * a : 48 + 16 * a + count, :] = value
    spread[96:97, :] = chain_row
    spread[97:98, :] = mask_row
    to_slots = (iota((rows, HALF), 1) // SLOTS == iota((rows, HALF), 0)).astype(F32)
    wide = dot(spread[...], to_slots, HIGH)
    slot = iota((1, HALF), 1) % SLOTS
    qb_ref[...] = jnp.zeros_like(qb_ref)
    scale = LOGIT_WEIGHT / math.sqrt(size)
    for h in range(heads):
        block = wide[h * size : (h + 1) * size, :] * scale
        qb_ref[2 * size * h : 2 * size * h + size, :] = jnp.where(slot == h, block, 0.0)
    qaux_ref[...] = jnp.zeros_like(qaux_ref)
    for a in range(3):
        for p in range(n_query):
            line = jnp.zeros((1, HALF), F32)
            for h in range(heads):
                at = 48 + 16 * a + h * n_query + p
                line = jnp.where(slot == h, wide[at : at + 1, :], line)
            qaux_ref[n_query * a + p : n_query * a + p + 1, :] = line
    raw = jnp.zeros((1, HALF), F32)
    bonus = jnp.zeros((1, HALF), F32)
    for h in range(heads):
        raw = jnp.where(slot == h, hw_ref[h], raw)
        bonus = jnp.where(slot == h, cb_ref[h], bonus)
    soft = jnp.maximum(raw, 0.0) + jnp.log1p(jnp.exp(-jnp.abs(raw)))
    used = 3 * n_query
    qaux_ref[used : used + 1, :] = soft * (math.sqrt(2.0 / (9.0 * n_query)) / 2.0)
    qaux_ref[used + 1 : used + 2, :] = bonus
    qaux_ref[used + 2 : used + 3, :] = wide[96:97, :]
    qaux_ref[used + 3 : used + 4, :] = wide[97:98, :]

    points[...] = jnp.zeros_like(points)
    points[0:12, :] = frames_ref[...]
    columns = points[...].T
    to_rows = (iota((HALF, rows), 0) // SLOTS == iota((HALF, rows), 1)).astype(F32)
    frows_ref[...] = dot(to_rows, columns, HIGH)


def bias_kernel(heads, pair_ref, wb_ref, bias_ref, weights):
    queries = pair_ref.shape[0]
    width = pair_ref.shape[3]
    keys = pair_ref.shape[1] * pair_ref.shape[2]
    lane = iota((width, HALF), 1)
    wb = wb_ref[...].astype(F32)
    each = jnp.zeros((width, HALF), F32)
    for h in range(heads):
        each = jnp.where(lane % SLOTS == h, wb[:, h : h + 1], each)
    for i in range(queries):
        weights[i * width : (i + 1) * width, :] = jnp.where(
            lane // SLOTS == i, each, 0.0
        ).astype(BF16)
    left = jnp.concatenate([pair_ref[i].reshape(keys, width) for i in range(queries)], axis=1)
    bias_ref[...] = dot(left, weights[...])


def attend_kernel(
    n_query, payload_ref, bias_ref, qb_ref, qaux_ref, pair_ref, part_ref, turned_w
):
    near, far, half, lanes = payload_ref.shape
    keys = near * far * half
    queries = pair_ref.shape[0]
    width = pair_ref.shape[3]
    block = jnp.concatenate(
        [payload_ref[k % near, k // near] for k in range(near * far)], axis=0
    )
    high = block[:, HALF:]
    first = high.astype(BF16)
    rest = high - first.astype(F32)
    second = rest.astype(BF16)
    third = (rest - second.astype(F32)).astype(BF16)
    split = jnp.concatenate([first, second, third], axis=1)

    row = iota((HALF, HALF), 0)
    lane = iota((HALF, HALF), 1)
    slot = lane % SLOTS

    def expanded(wanted):
        picks = (row == wanted).astype(F32).astype(BF16)
        return dot(split, jnp.concatenate([picks, picks, picks], axis=0))

    distance = jnp.zeros((keys, HALF), F32)
    for a in range(3):
        for p in range(n_query):
            wanted = jnp.where(slot < 3, COMP * a + 12 * slot + p, -1)
            at = n_query * a + p
            gap = qaux_ref[at : at + 1, :] - expanded(wanted)
            distance += gap * gap
    used = 3 * n_query
    scale = qaux_ref[used : used + 1, :]
    bonus = qaux_ref[used + 1 : used + 2, :]
    differ = expanded(jnp.full((HALF, HALF), CHAIN)) != qaux_ref[used + 2 : used + 3, :]
    there = expanded(jnp.full((HALF, HALF), PRESENT)) * qaux_ref[used + 3 : used + 4, :]
    logits = dot(block[:, :HALF], qb_ref[...], HIGH) + LOGIT_WEIGHT * (
        bias_ref[...] - scale * distance + jnp.where(differ, bonus, 0.0)
    )
    logits = logits - MASK_PENALTY * (1.0 - there)
    by_row = logits.T
    top = jnp.max(by_row, axis=1, keepdims=True)
    weights = jnp.exp(by_row - top)
    turned_w[...] = weights
    sums = dot(weights, block, HIGH)
    part_ref[:, HALF:] = jnp.where(iota((HALF, lanes), 1) == HALF + TOP, top, sums)
    upper = iota((2 * SLOTS, width), 0) < SLOTS
    for g in range(queries // 2):
        rows = slice(2 * SLOTS * g, 2 * SLOTS * (g + 1))
        right = jnp.concatenate(
            [pair_ref[2 * g].reshape(keys, width), pair_ref[2 * g + 1].reshape(keys, width)],
            axis=1,
        )
        both = dot(turned_w[rows, :].astype(BF16), right)
        part_ref[rows, 0:width] = jnp.where(upper, both[:, :width], both[:, width:])


def merge_kernel(
    heads,
    size,
    n_query,
    n_value,
    mine_ref,
    theirs_ref,
    frows_ref,
    w_out_ref,
    out_ref,
    small,
    large,
):
    copies, rows, _ = out_ref.shape
    tops = [ref[:, 2 * HALF + TOP : 2 * HALF + TOP + 1] for ref in (mine_ref, theirs_ref)]
    sums = [ref[:, 2 * HALF + ONE : 2 * HALF + ONE + 1] for ref in (mine_ref, theirs_ref)]
    best = jnp.maximum(tops[0], tops[1])
    factors = [jnp.exp(top - best) for top in tops]
    total = factors[0] * sums[0] + factors[1] * sums[1]
    merged = (mine_ref[...] * factors[0] + theirs_ref[...] * factors[1]) / total
    slot = iota((HALF, 1), 0) % SLOTS

    def of_own_head(first, step, count):
        picked = jnp.zeros((HALF, count), F32)
        for h in range(heads):
            at = first + step * h
            picked = jnp.where(slot == h, merged[:, at : at + count], picked)
        return picked

    attended = of_own_head(HALF + size, 2 * size, size)
    n_points = n_query + n_value
    moved = [
        of_own_head(2 * HALF + COMP * a + n_query, n_points, n_value)
        - frows_ref[:, 9 + a : 10 + a]
        for a in range(3)
    ]
    pointed = []
    for b in range(3):
        total_b = frows_ref[:, b : b + 1] * moved[0]
        for a in (1, 2):
            total_b += frows_ref[:, 3 * a + b : 3 * a + b + 1] * moved[a]
        pointed.append(total_b)
    norms = jnp.sqrt(
        pointed[0] * pointed[0] + pointed[1] * pointed[1] + pointed[2] * pointed[2] + 1.0
    )
    small[...] = jnp.zeros_like(small)
    small[:, 0:size] = attended
    for b in range(3):
        small[:, size + n_value * b : size + n_value * (b + 1)] = pointed[b]
    edge = size + 3 * n_value
    small[:, edge : edge + n_value] = norms
    source = iota((HALF, HALF), 0)
    target = iota((HALF, HALF), 1)
    inside = (source >= size) & (source < edge)
    goes = jnp.where(
        inside, size + 3 * ((source - size) % n_value) + (source - size) // n_value, source
    )
    order = (goes == target).astype(F32).astype(BF16)
    small[...] = dot(small[...].astype(BF16), order)
    large[...] = merged[:, :HALF]
    cut = edge + n_value
    update = jnp.zeros((rows, w_out_ref.shape[2]), F32)
    for h in range(heads):
        low = small[pl.ds(h, rows, stride=SLOTS), :].astype(BF16)
        update += dot(low[:, :cut], w_out_ref[h, 0:cut, :])
        wide = large[pl.ds(h, rows, stride=SLOTS), :].astype(BF16)
        update += dot(wide, w_out_ref[h, cut:, :])
    for k in range(copies):
        out_ref[k] = update


def finish_kernel(updates_ref, single_ref, gain_ref, wb_ref, frames_ref, out_ref, send_ref, flat):
    copies, rows, channels = updates_ref.shape
    mixed = single_ref[...].astype(F32)
    update = updates_ref[0]
    for k in range(1, copies):
        update += updates_ref[k]
    mixed = mixed + update
    centre = jnp.mean(mixed, axis=1, keepdims=True)
    away = mixed - centre
    spread = jnp.mean(away * away, axis=1, keepdims=True)
    gain = gain_ref[...].reshape(1, channels)
    single_out = (away * lax.rsqrt(spread + 1e-05) * gain).astype(BF16)
    out_ref[...] = single_out
    flat[...] = jnp.zeros_like(flat)
    flat[:, 0:6] = dot(single_out, wb_ref[...])
    motion = flat[...].T
    m = [motion[k : k + 1, :] for k in range(6)]
    qa = 1.0 / jnp.sqrt(1.0 + m[0] * m[0] + m[1] * m[1] + m[2] * m[2])
    qb, qc, qd = m[0] * qa, m[1] * qa, m[2] * qa
    spin = [
        [qa * qa + qb * qb - qc * qc - qd * qd, 2.0 * (qb * qc - qa * qd), 2.0 * (qb * qd + qa * qc)],
        [2.0 * (qb * qc + qa * qd), qa * qa - qb * qb + qc * qc - qd * qd, 2.0 * (qc * qd - qa * qb)],
        [2.0 * (qb * qd - qa * qc), 2.0 * (qc * qd + qa * qb), qa * qa - qb * qb - qc * qc + qd * qd],
    ]
    r = [[frames_ref[3 * a + b : 3 * a + b + 1, :] for b in range(3)] for a in range(3)]
    lines = []
    for a in range(3):
        for c in range(3):
            lines.append(r[a][0] * spin[0][c] + r[a][1] * spin[1][c] + r[a][2] * spin[2][c])
    for a in range(3):
        lines.append(
            frames_ref[9 + a : 10 + a, :] + (r[a][0] * m[3] + r[a][1] * m[4] + r[a][2] * m[5])
        )
    groups = HALF // rows
    repeat = (iota((rows, HALF), 1) % rows == iota((rows, HALF), 0)).astype(F32)
    wide = dot(jnp.concatenate(lines + lines[:4], axis=0), repeat, HIGH)
    group = iota((1, HALF), 1) // rows
    pieces = []
    for v in range(len(lines) // groups):
        piece = wide[groups * v : groups * v + 1, :]
        for s in range(1, groups):
            at = groups * v + s
            piece = jnp.where(group == s, wide[at : at + 1, :], piece)
        pieces.append(piece)
    line = jnp.concatenate(pieces, axis=1)
    send_ref[...] = jnp.broadcast_to(line, (send_ref.shape[0], line.shape[1])).reshape(
        send_ref.shape
    )


def spread_kernel(blocks_ref, out_ref):
    blocks, _, wide = blocks_ref.shape
    lines = out_ref.shape[0]
    rows = wide // lines
    groups = HALF // rows
    x = blocks_ref[...].reshape(blocks, wide)
    s = iota((blocks, HALF), 0) % groups
    g = iota((blocks, HALF), 1) // rows
    for v in range(wide // HALF):
        tile = x[:, HALF * v : HALF * (v + 1)]
        z = tile
        for d in range(1, groups):
            right = pltpu.roll(tile, rows * d, 1)
            up = pltpu.roll(right, blocks - d, 0)
            down = pltpu.roll(right, groups - d, 0)
            z = jnp.where(g - s == d, up, z)
            z = jnp.where(g - s == d - groups, down, z)
        for q in range(blocks // groups):
            out_ref[groups * v : groups * (v + 1), HALF * q : HALF * (q + 1)] = z[
                groups * q : groups * (q + 1), :
            ]


def call(kernel, outs, scratch=(), specs=None, n=0, cost=None, name=None):
    return pl.pallas_call(
        kernel,
        out_shape=outs,
        in_specs=specs or [VMEM] * n,
        out_specs=jax.tree.map(lambda _: VMEM, outs),
        scratch_shapes=list(scratch),
        cost_estimate=cost,
        name=name,
    )


def body(
    single,
    pair,
    frames,
    chain,
    mask,
    w_query,
    w_key_value,
    w_query_points,
    w_kv_points,
    w_pair_bias,
    head_weights,
    chain_bias,
    w_out,
    out_gain,
    w_backbone,
):
    rows, channels = single.shape
    blocks, half = pair.shape[1], pair.shape[2]
    width = pair.shape[3]
    heads = w_pair_bias.shape[1]
    size = w_query.shape[1] // heads
    n_query = w_query_points.shape[1] // (3 * heads)
    n_points = w_kv_points.shape[1] // (3 * heads)
    n_value = n_points - n_query
    keys = blocks * half
    shape = jax.ShapeDtypeStruct

    payload, qb, qaux, frows = call(
        functools.partial(project_kernel, heads, size, n_query, n_points),
        (
            shape((half, 2 * HALF), F32),
            shape((HALF, HALF), F32),
            shape((16, HALF), F32),
            shape((HALF, HALF), F32),
        ),
        (
            pltpu.VMEM((rows, 3 * HALF), F32),
            pltpu.VMEM((3 * HALF, rows), F32),
            pltpu.VMEM((HALF, rows), F32),
            pltpu.VMEM((rows, 2 * HALF), F32),
            pltpu.VMEM((104, rows), F32),
        ),
        specs=[VMEM] * 8 + [SMEM] * 2,
        name="project",
    )(
        single,
        frames,
        chain,
        mask,
        w_query,
        w_key_value,
        w_query_points,
        w_kv_points,
        head_weights,
        chain_bias,
    )
    gathered = lax.all_gather(payload, "far", axis=0, tiled=False)
    gathered = lax.all_gather(gathered, "near", axis=0, tiled=False)
    bias = call(
        functools.partial(bias_kernel, heads),
        shape((keys, HALF), F32),
        (pltpu.VMEM((rows * width, HALF), BF16),),
        n=2,
        name="bias",
    )(pair, w_pair_bias)
    part = call(
        functools.partial(attend_kernel, n_query),
        shape((HALF, 3 * HALF), F32),
        (pltpu.VMEM((HALF, keys), F32),),
        n=5,
        name="attend",
    )(gathered, bias, qb, qaux, pair)
    swap = [(k, 1 - k) for k in range(2)]
    other = lax.ppermute(part, "pair", swap)
    updates = call(
        functools.partial(merge_kernel, heads, size, n_query, n_value),
        shape((lax.axis_size("head"), rows, channels), F32),
        (pltpu.VMEM((HALF, HALF), F32), pltpu.VMEM((HALF, HALF), F32)),
        n=4,
        name="merge",
    )(part, other, frows, w_out)
    updates = lax.all_to_all(updates, "head", split_axis=0, concat_axis=0, tiled=True)
    single_out, send = call(
        finish_kernel,
        (shape((rows, channels), BF16), shape((blocks, 1, 12 * rows), F32)),
        (pltpu.VMEM((rows, HALF), F32),),
        n=5,
        name="finish",
    )(updates, single, out_gain, w_backbone, frames)
    received = lax.all_to_all(send, ("far", "near"), split_axis=0, concat_axis=0, tiled=True)
    frames_out = call(
        spread_kernel, shape((12, blocks * rows), F32), n=1, name="spread"
    )(received)
    return (single_out, frames_out)


def solution(mesh):
    groups, blocks, heads, pairs = (mesh.shape[a] for a in ("groups", "blk", "head", "pair"))
    near = 2 if blocks % 2 == 0 else 1
    finer = Mesh(
        mesh.devices.reshape(groups, blocks // near, near, heads, pairs),
        ("groups", "far", "near", "head", "pair"),
    )
    split = ("groups", "far", "near")
    placed = (
        P(split, None),
        P(split, None, "pair", None),
        P(None, split),
        P(split),
        P(split),
        P(None, "head"),
        P(None, "head"),
        P(None, "head"),
        P(None, "head"),
        P(None, "head"),
        P("head"),
        P("head"),
        P("head", None, None),
        P(),
        P(),
    )
    return jax.shard_map(
        body,
        mesh=finer,
        in_specs=placed,
        out_specs=(P(split, None), P(None, "groups")),
        check_vma=False,
    )
```

time: 170 us -> 160 us (0.941)
  blocking collectives: 140 us -> 115 us
  Pallas kernels: 0 us -> 19.7 us
  matrix products: 15 us -> 0 us
  waiting for transfers between devices: 0 us -> 7.15 us
  starting transfers between devices: 0 us -> 6.52 us
  other arithmetic: 3.57 us -> 0 us
    pallas_call x0 -> x6, Pallas kernels: none -> 19.7 us  [the longest x1 6.38 us: body(): call(functools.partial(attend_kernel, n_query), shape((HALF, 3 * HALF), F...]
    all_gather x1 -> x2, blocking collectives: 97.4 us -> 82 us  [the longest x1 74.9 us: body(): gathered = lax.all_gather(payload, 'far', axis=0, tiled=False)]
    dot_general x15 -> x0, matrix products: 15 us -> none  [the longest x1 3.88 us: to_local(): return jnp.einsum('abn,nhpa->nhpb', rotation, moved, precision=HIGH)]
    all_to_all x3 -> x1, blocking collectives: 43 us -> 33.3 us  [body(): lax.all_to_all(send, ('far', 'near'), split_axis=0, concat_axis=0, tiled=...]
    unnamed x25 -> x12, local copies, waits for them, and re-layouts: 0.43 us -> 9.78 us
    all_to_all x0 -> x1, waiting for transfers between devices: none -> 5.54 us  [body(): lax.all_to_all(updates, 'head', split_axis=0, concat_axis=0, tiled=True)]
    all_to_all x0 -> x1, starting transfers between devices: none -> 4.58 us  [body(): lax.all_to_all(updates, 'head', split_axis=0, concat_axis=0, tiled=True)]
    slice x24 -> x0, local copies, waits for them, and re-layouts: 2.76 us -> none  [the longest x15 1.27 us: joined_by_halves(): part[side::2]]
  transfers between devices with their start and end apart: 0 -> 2, of which waited for: 0 -> 2; matrix products, arithmetic and copies ran while one was open for 0% -> 0% of each run, Pallas kernels for 0% -> 0%
where the time goes in v1:
time: 160 us; the launch traced here: 159 us
  blocking collectives  115 us (72%)
  Pallas kernels  19.7 us (12%)
  local copies, waits for them, and re-layouts  9.78 us (6%)
  waiting for transfers between devices  7.15 us (4%)
  starting transfers between devices  6.52 us (4%)
    all_gather x1, blocking collectives, body(): gathered = lax.all_gather(payload, 'far', axis=0, tiled=False)  74.9 us
    all_to_all x1, blocking collectives, body(): lax.all_to_all(send, ('far', 'near'), split_axis=0, concat_axis=0, tiled=...  33.3 us
    unnamed x12, local copies, waits for them, and re-layouts  9.78 us
    all_gather x1, blocking collectives, body(): gathered = lax.all_gather(gathered, 'near', axis=0, tiled=False)  7.15 us
    pallas_call x1, Pallas kernels, body(): call(functools.partial(attend_kernel, n_query), shape((HALF, 3 * HALF), F...  6.38 us
    all_to_all x1, waiting for transfers between devices, body(): lax.all_to_all(updates, 'head', split_axis=0, concat_axis=0, tiled=True)  5.54 us
    all_to_all x1, starting transfers between devices, body(): lax.all_to_all(updates, 'head', split_axis=0, concat_axis=0, tiled=True)  4.58 us
    pallas_call x1, Pallas kernels, body(): call(functools.partial(bias_kernel, heads), shape((keys, HALF), F32), (pl...  4.24 us
  transfers between devices with their start and end apart: 2, of which 2 were waited for; matrix products, arithmetic and copies ran while one was open for 0% of the time, Pallas kernels for 0%

profile of v1, /device:TPU:40, one launch (start us, length us, event | category | flops | bytes accessed | tf_op | source)
XLA Modules:
  0.0 159.2 jit_solution(7869917080654250477)
XLA Ops:
  0.6 1.5 copy.23.wq_ref
  2.1 1.6 %copy.24.wkv_ref = bf16[384,96]{1,0:T(8,128)(2,1)} copy(bf16[384,96]{0,1:T(8,128)(2,1)} %param.21) | data formatting | bytes 147456 | tf_op args[6]
  3.7 1.5 copy.25.wqp_ref
  5.3 1.6 %copy.26.wkp_ref = bf16[384,108]{1,0:T(8,128)(2,1)} copy(bf16[384,108]{0,1:T(8,128)(2,1)} %param.23) | data formatting | bytes 165888 | tf_op args[8]
  6.9 2.4 %project.1 = (f32[16,256]{1,0:T(8,128)}, f32[128,128]{1,0:T(8,128)}, f32[16,128]{1,0:T(8,128)}, f32[128,128]{1,0:T(8,128)}) custom-call(bf16[32,384]{1,0:T(8,128)(2,1)} %single_ref.3, f32[12,32]{1,0:T(8,128)} %frames_ref.3, s32[32]{0:T(128)} %chain_ref.1, s32[32]{0:T(128)} %mask_ref.1, bf16[384,48]{1,0:T(8,128)(2,1)} %copy.23.wq_ref, ...), custom_call_target="tpu_custom_call" | custom-call | tf_op jit(solution)/shard_map/project/pallas_call | solution.py:398
  9.2 74.9 %all-gather = f32[256,256]{1,0:T(8,128)S(1)} all-gather(f32[16,256]{1,0:T(8,128)} %get-tuple-element.8), channel_id=2, replica_groups=mesh['groups'=2,'far'=16,'near'=2,'head'=4,'pair'=2] {'far'}, dimensions={0}, use_global_device_ids=true | all-gather | bytes 278528 | tf_op jit(solution)/shard_map/all_gather | solution.py:427
  84.1 7.1 %all-gather.1 = f32[32,16,256]{2,1,0:T(8,128)} all-gather(f32[16,16,256]{2,1,0:T(8,128)S(1)} %bitcast.3), channel_id=3, replica_groups=mesh['groups'=2,'far'=16,'near'=2,'head'=4,'pair'=2] {'near'}, dimensions={0}, use_global_device_ids=true | all-gather | bytes 786432 | tf_op jit(solution)/shard_map/all_gather | solution.py:428
  91.3 1.4 copy.27.wb_ref
  92.7 4.2 %bias.1.bias_ref = f32[512,128]{1,0:T(8,128)} custom-call(bf16[32,32,16,128]{3,2,1,0:T(8,128)(2,1)} %pair_ref.3, bf16[128,3]{1,0:T(8,128)(2,1)} %copy.27.wb_ref), custom_call_target="tpu_custom_call" | custom-call | tf_op jit(solution)/shard_map/bias/pallas_call | solution.py:429
  96.9 0.0 copy-start.2
  96.9 6.4 %attend.1.mine_ref = f32[128,384]{1,0:T(8,128)} custom-call(f32[2,16,16,256]{3,2,1,0:T(8,128)} %bitcast.2, f32[512,128]{1,0:T(8,128)} %bias.1.bias_ref, f32[128,128]{1,0:T(8,128)} %get-tuple-element.9.qb_ref, f32[16,128]{1,0:T(8,128)} %get-tuple-element.10.qaux_ref, bf16[32,32,16,128]{3,2,1,0:T(8,128)(2,1)} %pair_ref.3), custom_call_target="tpu_custom_call" | custom-call | tf_op jit(solution)/shard_map/attend/pallas_call | solution.py:436
  103.3 1.9 %collective-permute-start = (f32[128,384]{1,0:T(8,128)}, f32[128,384]{1,0:T(8,128)S(1)}, u32[]{:S(2)}, u32[]{:S(2)}) collective-permute-start(f32[128,384]{1,0:T(8,128)} %attend.1.mine_ref), channel_id=1, source_target_pairs={{0,1},{1,0},{2,3},{3,2},{4,5},{5,4},{6,7},{7,6},{8,9},{9,8},{10,11... | collective-permute-start | bytes 589832 | tf_op jit(solution)/shard_map/ppermute | solution.py:444
  105.2 1.6 %collective-permute-done.theirs_ref = f32[128,384]{1,0:T(8,128)S(1)} collective-permute-done((f32[128,384]{1,0:T(8,128)}, f32[128,384]{1,0:T(8,128)S(1)}, u32[]{:S(2)}, u32[]{:S(2)}) %collective-permute-start) | collective-permute-done | bytes 196640 | tf_op jit(solution)/shard_map/ppermute | solution.py:444
  106.9 0.0 copy-start.1
  106.9 0.7 copy-done.1
  107.5 3.0 %merge.1 = f32[4,32,384]{2,1,0:T(8,128)} custom-call(f32[128,384]{1,0:T(8,128)} %attend.1.mine_ref, f32[128,384]{1,0:T(8,128)} %copy-done.1, f32[128,128]{1,0:T(8,128)} %get-tuple-element.11.frows_ref, bf16[3,176,384]{2,1,0:T(8,128)(2,1)} %w_out_ref.1), custom_call_target="tpu_custom_call" | custom-call | tf_op jit(solution)/shard_map/merge/pallas_call | solution.py:445
  110.5 4.6 %all-to-all-start = ((f32[4,32,384]{2,1,0:T(8,128)}), f32[4,32,384]{2,1,0:T(8,128)S(1)}, u32[]{:S(2)}, u32[]{:S(2)}) async-start(f32[4,32,384]{2,1,0:T(8,128)} %merge.1), calls=%async_computation | async-start | bytes 393216 | tf_op jit(solution)/shard_map/all_to_all | solution.py:452
  115.1 0.0 copy-done.2
  115.1 0.8 copy.28.wb_ref
  115.9 5.5 %all-to-all-done.updates_ref = f32[4,32,384]{2,1,0:T(8,128)S(1)} async-done(((f32[4,32,384]{2,1,0:T(8,128)}), f32[4,32,384]{2,1,0:T(8,128)S(1)}, u32[]{:S(2)}, u32[]{:S(2)}) %all-to-all-start) | async-done | bytes 196640 | tf_op jit(solution)/shard_map/all_to_all | solution.py:452
  121.4 0.0 copy-start
  121.4 0.7 copy-done
  122.1 2.2 %finish.1 = (bf16[32,384]{1,0:T(8,128)(2,1)}, f32[32,1,384]{2,1,0:T(1,128)}) custom-call(f32[4,32,384]{2,1,0:T(8,128)} %copy-done, bf16[32,384]{1,0:T(8,128)(2,1)} %single_ref.3, f32[384]{0:T(512)} %gain_ref.1, bf16[384,6]{1,0:T(8,128)(2,1)} %copy.28.wb_ref, f32[12,32]{1,0:T(8,128)} %frames_ref.3), custom_call_target="tpu_custom_call" | custom-call | tf_op jit(solution)/shard_map/finish/pallas_call | solution.py:453
  124.3 33.3 %all_to_all.10.blocks_ref = f32[32,1,384]{2,1,0:T(1,128)} all-to-all(f32[32,1,384]{2,1,0:T(1,128)} %get-tuple-element.13), channel_id=1, replica_groups=mesh['groups'=2,'far'=16,'near'=2,'head'=4,'pair'=2] {'far','near'}, dimensions={0} | all-to-all | bytes 98304 | tf_op jit(solution)/shard_map/all_to_all | solution.py:460
  157.6 1.5 spread.1
Async XLA Ops:
  96.9 18.2 %copy-start.2 = (bf16[384,6]{0,1:T(8,128)(2,1)S(1)}, bf16[384,6]{0,1:T(8,128)(2,1)}, u32[]{:S(2)}) copy-start(bf16[384,6]{0,1:T(8,128)(2,1)} %param.29) | copy-start | bytes 13828
  103.3 3.6 %collective-permute-start = (f32[128,384]{1,0:T(8,128)}, f32[128,384]{1,0:T(8,128)S(1)}, u32[]{:S(2)}, u32[]{:S(2)}) collective-permute-start(f32[128,384]{1,0:T(8,128)} %attend.1.mine_ref), channel_id=1, source_target_pairs={{0,1},{1,0},{2,3},{3,2},{4,5},{5,4},{6,7},{7,6},{8,9},{9,8},{10,11... | collective-permute-start | bytes 589832 | tf_op jit(solution)/shard_map/ppermute | solution.py:444
  106.9 0.7 copy-start.1
  110.5 10.9 %all-to-all-start = ((f32[4,32,384]{2,1,0:T(8,128)}), f32[4,32,384]{2,1,0:T(8,128)S(1)}, u32[]{:S(2)}, u32[]{:S(2)}) async-start(f32[4,32,384]{2,1,0:T(8,128)} %merge.1), calls=%async_computation | async-start | bytes 393216 | tf_op jit(solution)/shard_map/all_to_all | solution.py:452
  121.4 0.7 copy-start

commit v2 on v1

--- a/solution.py
+++ b/solution.py
@@ -17,10 +17,11 @@
 
 SLOTS = 4
 HALF = 128
+BIAS_STEPS = 4
 COMP = 40
 CHAIN, PRESENT, ONE, TOP = 120, 121, 122, 123
 VMEM = pl.BlockSpec(memory_space=pltpu.VMEM)
-SMEM = pl.BlockSpec(memory_space=pltpu.SMEM)
+HBM = pl.BlockSpec(memory_space=pltpu.HBM)
 
 
 def iota(shape, dim):
@@ -29,6 +30,10 @@
 
 def dot(a, b, precision=None):
     return jnp.dot(a, b, preferred_element_type=F32, precision=precision)
+
+
+def dot_nt(a, b):
+    return lax.dot_general(a, b, (((1,), (1,)), ((), ())), preferred_element_type=F32)
 
 
 def rotated(frames_ref, parts):
@@ -46,44 +51,38 @@
     size,
     n_query,
     n_points,
-    single_ref,
-    frames_ref,
-    chain_ref,
-    mask_ref,
-    wq_ref,
-    wkv_ref,
-    wqp_ref,
-    wkp_ref,
-    hw_ref,
-    cb_ref,
-    payload_ref,
-    qb_ref,
-    qaux_ref,
-    frows_ref,
-    flat,
-    turned,
-    points,
-    full,
-    spread,
+    *refs,
 ):
+    sources, refs = refs[:10], refs[10:]
+    payload_ref, qb_ref, qaux_ref, frows_ref, turned, points, full, spread = refs[:8]
+    local_refs, sem = refs[8:18], refs[18]
+    copies = [
+        pltpu.make_async_copy(source, target, sem.at[k])
+        for k, (source, target) in enumerate(zip(sources, local_refs))
+    ]
+    for copy in copies:
+        copy.start()
+    single_ref, frames_ref, chain_ref, mask_ref, wq_ref, wkv_ref, wqp_ref, wkp_ref = local_refs[:8]
+    hw_ref, cb_ref = local_refs[8:]
+    full[...] = jnp.zeros_like(full)
+    points[...] = jnp.zeros_like(points)
+    spread[...] = jnp.zeros_like(spread)
+    qb_ref[...] = jnp.zeros_like(qb_ref)
+    qaux_ref[...] = jnp.zeros_like(qaux_ref)
+    for copy in copies:
+        copy.wait()
     rows = single_ref.shape[0]
     half = payload_ref.shape[0]
     x = single_ref[...]
     q_wide = heads * size
-    flat[...] = jnp.zeros_like(flat)
-    flat[:, 0:q_wide] = dot(x, wq_ref[...])
-    flat[:, HALF : HALF + 3 * heads * n_query] = dot(x, wqp_ref[...])
-    flat[:, 2 * HALF : 2 * HALF + 3 * heads * n_points] = dot(x, wkp_ref[...])
-    full[...] = jnp.zeros_like(full)
-    full[:, 0 : 2 * q_wide] = dot(x, wkv_ref[...])
-    for k in range(3):
-        turned[k * HALF : (k + 1) * HALF, :] = flat[:, k * HALF : (k + 1) * HALF].T
+    turned[HALF : HALF + 3 * heads * n_query, :] = dot_nt(wqp_ref[...], x)
+    turned[2 * HALF : 2 * HALF + 3 * heads * n_points, :] = dot_nt(wkp_ref[...], x)
+    full[:, 0 : 2 * q_wide] = dot_nt(x, wkv_ref[...])
     chain_row = chain_ref[...].astype(F32).reshape(1, rows)
     mask_row = mask_ref[...].astype(F32).reshape(1, rows)
 
     count = heads * n_points
     local = [turned[pl.ds(2 * HALF + b, count, stride=3), :] for b in range(3)]
-    points[...] = jnp.zeros_like(points)
     for a, value in enumerate(rotated(frames_ref, local)):
         points[COMP * a : COMP * a + count, :] = value
     points[CHAIN : CHAIN + 1, :] = chain_row
@@ -95,8 +94,7 @@
 
     count = heads * n_query
     local = [turned[pl.ds(HALF + b, count, stride=3), :] for b in range(3)]
-    spread[...] = jnp.zeros_like(spread)
-    spread[0:q_wide, :] = turned[0:q_wide, :]
+    spread[0:q_wide, :] = dot_nt(wq_ref[...], x)
     for a, value in enumerate(rotated(frames_ref, local)):
         spread[48 + 16 * a : 48 + 16 * a + count, :] = value
     spread[96:97, :] = chain_row
@@ -104,12 +102,10 @@
     to_slots = (iota((rows, HALF), 1) // SLOTS == iota((rows, HALF), 0)).astype(F32)
     wide = dot(spread[...], to_slots, HIGH)
     slot = iota((1, HALF), 1) % SLOTS
-    qb_ref[...] = jnp.zeros_like(qb_ref)
     scale = LOGIT_WEIGHT / math.sqrt(size)
     for h in range(heads):
         block = wide[h * size : (h + 1) * size, :] * scale
         qb_ref[2 * size * h : 2 * size * h + size, :] = jnp.where(slot == h, block, 0.0)
-    qaux_ref[...] = jnp.zeros_like(qaux_ref)
     for a in range(3):
         for p in range(n_query):
             line = jnp.zeros((1, HALF), F32)
@@ -136,33 +132,51 @@
     frows_ref[...] = dot(to_rows, columns, HIGH)
 
 
-def bias_kernel(heads, pair_ref, wb_ref, bias_ref, weights):
+def bias_kernel(heads, pair_ref, wb_hbm, bias_ref, here_ref, weights, wb_ref, sem):
     queries = pair_ref.shape[0]
     width = pair_ref.shape[3]
     keys = pair_ref.shape[1] * pair_ref.shape[2]
+    each_step = queries // BIAS_STEPS
+    copies = []
+    for k in range(BIAS_STEPS):
+        part = pl.ds(k * each_step, each_step)
+        copies.append(pltpu.make_async_copy(pair_ref.at[part], here_ref.at[part], sem.at[k]))
+        copies[k].start()
+    small = pltpu.make_async_copy(wb_hbm, wb_ref, sem.at[BIAS_STEPS])
+    small.start()
     lane = iota((width, HALF), 1)
+    row = iota((HALF, width), 0)
+    small.wait()
     wb = wb_ref[...].astype(F32)
-    each = jnp.zeros((width, HALF), F32)
+    each = jnp.zeros((HALF, width), F32)
     for h in range(heads):
-        each = jnp.where(lane % SLOTS == h, wb[:, h : h + 1], each)
+        each = jnp.where(row % SLOTS == h, wb[h : h + 1, :], each)
+    each = each.T
     for i in range(queries):
         weights[i * width : (i + 1) * width, :] = jnp.where(
             lane // SLOTS == i, each, 0.0
         ).astype(BF16)
-    left = jnp.concatenate([pair_ref[i].reshape(keys, width) for i in range(queries)], axis=1)
-    bias_ref[...] = dot(left, weights[...])
+    for k in range(BIAS_STEPS):
+        copies[k].wait()
+        these = range(k * each_step, (k + 1) * each_step)
+        left = jnp.concatenate([here_ref[i].reshape(keys, width) for i in these], axis=1)
+        found = dot(left, weights[these[0] * width : (these[-1] + 1) * width, :])
+        bias_ref[...] = found if k == 0 else bias_ref[...] + found
 
 
 def attend_kernel(
-    n_query, payload_ref, bias_ref, qb_ref, qaux_ref, pair_ref, part_ref, turned_w
+    n_query, mine_ref, across_ref, bias_ref, qb_ref, qaux_ref, pair_ref, part_ref, turned_w, block
 ):
-    near, far, half, lanes = payload_ref.shape
-    keys = near * far * half
+    far, half, lanes = mine_ref.shape
+    keys = 2 * far * half
     queries = pair_ref.shape[0]
     width = pair_ref.shape[3]
-    block = jnp.concatenate(
-        [payload_ref[k % near, k // near] for k in range(near * far)], axis=0
-    )
+    place = lax.axis_index("near")
+    for k in range(far):
+        start = pl.multiple_of((2 * k + place) * half, half)
+        block[pl.ds(start, half), :] = mine_ref[k]
+        start = pl.multiple_of((2 * k + 1 - place) * half, half)
+        block[pl.ds(start, half), :] = across_ref[k]
     high = block[:, HALF:]
     first = high.astype(BF16)
     rest = high - first.astype(F32)
@@ -198,7 +212,7 @@
     top = jnp.max(by_row, axis=1, keepdims=True)
     weights = jnp.exp(by_row - top)
     turned_w[...] = weights
-    sums = dot(weights, block, HIGH)
+    sums = dot(weights, block[...], HIGH)
     part_ref[:, HALF:] = jnp.where(iota((HALF, lanes), 1) == HALF + TOP, top, sums)
     upper = iota((2 * SLOTS, width), 0) < SLOTS
     for g in range(queries // 2):
@@ -282,7 +296,7 @@
         out_ref[k] = update
 
 
-def finish_kernel(updates_ref, single_ref, gain_ref, wb_ref, frames_ref, out_ref, send_ref, flat):
+def finish_kernel(updates_ref, single_ref, gain_ref, wb_ref, frames_ref, out_ref, send_ref):
     copies, rows, channels = updates_ref.shape
     mixed = single_ref[...].astype(F32)
     update = updates_ref[0]
@@ -295,9 +309,7 @@
     gain = gain_ref[...].reshape(1, channels)
     single_out = (away * lax.rsqrt(spread + 1e-05) * gain).astype(BF16)
     out_ref[...] = single_out
-    flat[...] = jnp.zeros_like(flat)
-    flat[:, 0:6] = dot(single_out, wb_ref[...])
-    motion = flat[...].T
+    motion = dot_nt(wb_ref[...], single_out)
     m = [motion[k : k + 1, :] for k in range(6)]
     qa = 1.0 / jnp.sqrt(1.0 + m[0] * m[0] + m[1] * m[1] + m[2] * m[2])
     qb, qc, qd = m[0] * qa, m[1] * qa, m[2] * qa
@@ -355,7 +367,11 @@
             ]
 
 
-def call(kernel, outs, scratch=(), specs=None, n=0, cost=None, name=None):
+def in_hbm(x):
+    return pltpu.with_memory_space_constraint(x, pltpu.HBM)
+
+
+def call(kernel, outs, scratch=(), specs=None, n=0, room=4, cost=None, name=None):
     return pl.pallas_call(
         kernel,
         out_shape=outs,
@@ -363,6 +379,7 @@
         out_specs=jax.tree.map(lambda _: VMEM, outs),
         scratch_shapes=list(scratch),
         cost_estimate=cost,
+        compiler_params=pltpu.CompilerParams(vmem_limit_bytes=room * 1024 * 1024),
         name=name,
     )
 
@@ -395,6 +412,18 @@
     keys = blocks * half
     shape = jax.ShapeDtypeStruct
 
+    inputs = (
+        single,
+        frames,
+        chain,
+        mask,
+        w_query.T,
+        w_key_value.T,
+        w_query_points.T,
+        w_kv_points.T,
+        head_weights,
+        chain_bias,
+    )
     payload, qb, qaux, frows = call(
         functools.partial(project_kernel, heads, size, n_query, n_points),
         (
@@ -404,43 +433,41 @@
             shape((HALF, HALF), F32),
         ),
         (
-            pltpu.VMEM((rows, 3 * HALF), F32),
             pltpu.VMEM((3 * HALF, rows), F32),
             pltpu.VMEM((HALF, rows), F32),
             pltpu.VMEM((rows, 2 * HALF), F32),
             pltpu.VMEM((104, rows), F32),
+            *(pltpu.VMEM(x.shape, x.dtype) for x in inputs[:8]),
+            *(pltpu.SMEM(x.shape, x.dtype) for x in inputs[8:]),
+            pltpu.SemaphoreType.DMA((len(inputs),)),
         ),
-        specs=[VMEM] * 8 + [SMEM] * 2,
+        specs=[HBM] * len(inputs),
         name="project",
-    )(
-        single,
-        frames,
-        chain,
-        mask,
-        w_query,
-        w_key_value,
-        w_query_points,
-        w_kv_points,
-        head_weights,
-        chain_bias,
-    )
+    )(*(in_hbm(x) for x in inputs))
     gathered = lax.all_gather(payload, "far", axis=0, tiled=False)
-    gathered = lax.all_gather(gathered, "near", axis=0, tiled=False)
-    bias = call(
+    swap = [(k, 1 - k) for k in range(2)]
+    across = lax.ppermute(gathered, "near", swap)
+    bias, pair_here = call(
         functools.partial(bias_kernel, heads),
-        shape((keys, HALF), F32),
-        (pltpu.VMEM((rows * width, HALF), BF16),),
-        n=2,
+        (shape((keys, HALF), F32), shape(pair.shape, pair.dtype)),
+        (
+            pltpu.VMEM((rows * width, HALF), BF16),
+            pltpu.VMEM((heads, width), w_pair_bias.dtype),
+            pltpu.SemaphoreType.DMA((BIAS_STEPS + 1,)),
+        ),
+        specs=[HBM, HBM],
+        room=16,
+        cost=pl.CostEstimate(flops=10**9, bytes_accessed=2 * pair.size, transcendentals=0),
         name="bias",
-    )(pair, w_pair_bias)
+    )(in_hbm(pair), in_hbm(w_pair_bias.T))
     part = call(
         functools.partial(attend_kernel, n_query),
         shape((HALF, 3 * HALF), F32),
-        (pltpu.VMEM((HALF, keys), F32),),
-        n=5,
+        (pltpu.VMEM((HALF, keys), F32), pltpu.VMEM((keys, 2 * HALF), F32)),
+        n=6,
+        room=24,
         name="attend",
-    )(gathered, bias, qb, qaux, pair)
-    swap = [(k, 1 - k) for k in range(2)]
+    )(gathered, across, bias, qb, qaux, pair_here)
     other = lax.ppermute(part, "pair", swap)
     updates = call(
         functools.partial(merge_kernel, heads, size, n_query, n_value),
@@ -453,10 +480,9 @@
     single_out, send = call(
         finish_kernel,
         (shape((rows, channels), BF16), shape((blocks, 1, 12 * rows), F32)),
-        (pltpu.VMEM((rows, HALF), F32),),
         n=5,
         name="finish",
-    )(updates, single, out_gain, w_backbone, frames)
+    )(updates, single, out_gain, w_backbone.T, frames)
     received = lax.all_to_all(send, ("far", "near"), split_axis=0, concat_axis=0, tiled=True)
     frames_out = call(
         spread_kernel, shape((12, blocks * rows), F32), n=1, name="spread"
@@ -466,7 +492,7 @@
 
 def solution(mesh):
     groups, blocks, heads, pairs = (mesh.shape[a] for a in ("groups", "blk", "head", "pair"))
-    near = 2 if blocks % 2 == 0 else 1
+    near = 2
     finer = Mesh(
         mesh.devices.reshape(groups, blocks // near, near, heads, pairs),
         ("groups", "far", "near", "head", "pair"),

time: 160 us -> 139 us (0.87)
  local copies, waits for them, and re-layouts: 9.78 us -> 0.03 us
  Pallas kernels: 19.7 us -> 12.6 us
  waiting for transfers between devices: 7.15 us -> 1.41 us
  blocking collectives: 115 us -> 118 us
    all_to_all x0 -> x1, blocking collectives: none -> 10.8 us  [body(): lax.all_to_all(updates, 'head', split_axis=0, concat_axis=0, tiled=True)]
    unnamed x12 -> x10, local copies, waits for them, and re-layouts: 9.78 us -> 0.03 us
    all_gather x1 -> x0, blocking collectives: 7.15 us -> none  [body(): gathered = lax.all_gather(gathered, 'near', axis=0, tiled=False)]
    all_to_all x1 -> x0, waiting for transfers between devices: 5.54 us -> none  [body(): lax.all_to_all(updates, 'head', split_axis=0, concat_axis=0, tiled=True)]
    all_to_all x1 -> x0, starting transfers between devices: 4.58 us -> none  [body(): lax.all_to_all(updates, 'head', split_axis=0, concat_axis=0, tiled=True)]
    ppermute x0 -> x1, starting transfers between devices: none -> 3.71 us  [body(): across = lax.ppermute(gathered, 'near', swap)]
    pallas_call x1, Pallas kernels: 6.38 us -> 3.31 us  [body(): call(functools.partial(attend_kernel, n_query), shape((HALF, 3 * HALF), F...]
    pallas_call x1, Pallas kernels: 2.98 us -> 1.07 us  [body(): call(functools.partial(merge_kernel, heads, size, n_query, n_value), shap...]
  transfers between devices with their start and end apart: 2 -> 2, of which waited for: 2 -> 1; matrix products, arithmetic and copies ran while one was open for 0% -> 0% of each run, Pallas kernels for 0% -> 3%
where the time goes in v2:
time: 139 us
  blocking collectives  118 us (85%)
  Pallas kernels  12.6 us (9%)
  starting transfers between devices  5.66 us (4%)
  waiting for transfers between devices  1.41 us (1%)
    all_gather x1, blocking collectives, body(): gathered = lax.all_gather(payload, 'far', axis=0, tiled=False)  74.5 us
    all_to_all x1, blocking collectives, body(): lax.all_to_all(send, ('far', 'near'), split_axis=0, concat_axis=0, tiled=...  33 us
    all_to_all x1, blocking collectives, body(): lax.all_to_all(updates, 'head', split_axis=0, concat_axis=0, tiled=True)  10.8 us
    pallas_call x1, Pallas kernels, body(): call(functools.partial(bias_kernel, heads), (shape((keys, HALF), F32), sh...  4.85 us
    ppermute x1, starting transfers between devices, body(): across = lax.ppermute(gathered, 'near', swap)  3.71 us
    pallas_call x1, Pallas kernels, body(): call(functools.partial(attend_kernel, n_query), shape((HALF, 3 * HALF), F...  3.31 us
  transfers between devices with their start and end apart: 2, of which 1 were waited for; matrix products, arithmetic and copies ran while one was open for 0% of the time, Pallas kernels for 3%

profile of v2, /device:TPU:40, one launch (start us, length us, event | category | flops | bytes accessed | tf_op | source)
XLA Modules:
  0.0 138.7 jit_solution(18083623242373338156)
XLA Ops:
  0.6 1.7 %project.1 = (f32[16,256]{1,0:T(8,128)S(1)}, f32[128,128]{1,0:T(8,128)S(1)}, f32[16,128]{1,0:T(8,128)S(1)}, f32[128,128]{1,0:T(8,128)S(1)}) custom-call(bf16[32,384]{1,0:T(8,128)(2,1)} %single_ref.1, f32[12,32]{1,0:T(8,128)} %frames_ref.1, s32[32]{0:T(128)} %refs_2_.1, s32[32]{0:T(128)} %refs_3_.1, bf16[48,384]{1,0:T(8,128)(2,1)} %bitcast.12, ...), custom_call_target="tpu_custom_call" | custom-call | tf_op jit(solution)/shard_map/project/pallas_call | solution.py:427
  2.3 74.5 %all-gather = f32[256,256]{1,0:T(8,128)S(1)} all-gather(f32[16,256]{1,0:T(8,128)S(1)} %get-tuple-element.10), channel_id=2, replica_groups=mesh['groups'=2,'far'=16,'near'=2,'head'=4,'pair'=2] {'far'}, dimensions={0}, use_global_device_ids=true | all-gather | bytes 278528 | tf_op jit(solution)/shard_map/all_gather | solution.py:447
  76.8 3.7 %collective-permute-start = (f32[16,16,256]{2,1,0:T(8,128)S(1)}, f32[16,16,256]{2,1,0:T(8,128)S(1)}, u32[]{:S(2)}, u32[]{:S(2)}) collective-permute-start(f32[16,16,256]{2,1,0:T(8,128)S(1)} %bitcast.7), channel_id=1, source_target_pairs={{0,8},{8,0},{1,9},{9,1},{2,10},{10,2},{3,11},{11,3},{4,12},{12,4},... | collective-permute-start | bytes 786440 | tf_op jit(solution)/shard_map/ppermute | solution.py:449
  80.5 0.0 copy-start
  80.6 4.8 %bias.1 = (f32[512,128]{1,0:T(8,128)S(1)}, bf16[32,32,16,128]{3,2,1,0:T(8,128)(2,1)S(1)}) custom-call(bf16[32,32,16,128]{3,2,1,0:T(8,128)(2,1)} %pair_ref.1, bf16[3,128]{1,0:T(4,128)(2,1)} %bitcast.14), custom_call_target="tpu_custom_call" | custom-call | flops 1000000000 | bytes 4194304 | tf_op jit(solution)/shard_map/bias/pallas_call | solution.py:450
  85.4 0.0 copy-start.1
  85.4 0.0 copy-start.2
  85.4 0.0 copy-start.3
  85.4 0.0 copy-start.4
  85.5 0.0 collective-permute-done.across_ref
  85.5 3.3 %attend.1.mine_ref = f32[128,384]{1,0:T(8,128)S(1)} custom-call(f32[16,16,256]{2,1,0:T(8,128)S(1)} %bitcast.8, f32[16,16,256]{2,1,0:T(8,128)S(1)} %collective-permute-done.across_ref, f32[512,128]{1,0:T(8,128)S(1)} %get-tuple-element.11.bias_ref, f32[128,128]{1,0:T(8,128)S(1)} %get-tuple-element.12.qb_ref, f32[16,128]{1,0:T(8,128)S(1)} %get-tuple-element.13.qaux_ref, ...), custom_call_target="tpu_custom_call" | custom-call | tf_op jit(solution)/shard_map/attend/pallas_call | solution.py:463
  88.8 2.0 %collective-permute-start.1 = (f32[128,384]{1,0:T(8,128)S(1)}, f32[128,384]{1,0:T(8,128)S(1)}, u32[]{:S(2)}, u32[]{:S(2)}) collective-permute-start(f32[128,384]{1,0:T(8,128)S(1)} %attend.1.mine_ref), channel_id=1, source_target_pairs={{0,1},{1,0},{2,3},{3,2},{4,5},{5,4},{6,7},{7,6},{8,9},{9,8},{10,11... | collective-permute-start | bytes 589832 | tf_op jit(solution)/shard_map/ppermute | solution.py:471
  90.7 1.4 %collective-permute-done.1.theirs_ref = f32[128,384]{1,0:T(8,128)S(1)} collective-permute-done((f32[128,384]{1,0:T(8,128)S(1)}, f32[128,384]{1,0:T(8,128)S(1)}, u32[]{:S(2)}, u32[]{:S(2)}) %collective-permute-start.1) | collective-permute-done | bytes 196640 | tf_op jit(solution)/shard_map/ppermute | solution.py:471
  92.2 0.0 copy-done
  92.2 1.1 merge.1
  93.2 10.8 %all_to_all.10.updates_ref = f32[4,32,384]{2,1,0:T(8,128)S(1)} all-to-all(f32[4,32,384]{2,1,0:T(8,128)S(1)} %merge.1), channel_id=1, replica_groups=mesh['groups'=2,'far'=16,'near'=2,'head'=4,'pair'=2] {'head'}, dimensions={0} | all-to-all | bytes 393216 | tf_op jit(solution)/shard_map/all_to_all | solution.py:479
  104.0 0.0 copy-done.1
  104.0 0.0 copy-done.2
  104.0 0.0 copy-done.3
  104.0 0.0 copy-done.4
  104.0 0.9 finish.1
  104.9 33.0 %all_to_all.11.blocks_ref = f32[32,1,384]{2,1,0:T(1,128)S(1)} all-to-all(f32[32,1,384]{2,1,0:T(1,128)S(1)} %get-tuple-element.17), channel_id=1, replica_groups=mesh['groups'=2,'far'=16,'near'=2,'head'=4,'pair'=2] {'far','near'}, dimensions={0} | all-to-all | bytes 98304 | tf_op jit(solution)/shard_map/all_to_all | solution.py:486
  137.9 0.7 spread.1
Async XLA Ops:
  76.8 8.6 %collective-permute-start = (f32[16,16,256]{2,1,0:T(8,128)S(1)}, f32[16,16,256]{2,1,0:T(8,128)S(1)}, u32[]{:S(2)}, u32[]{:S(2)}) collective-permute-start(f32[16,16,256]{2,1,0:T(8,128)S(1)} %bitcast.7), channel_id=1, source_target_pairs={{0,8},{8,0},{1,9},{9,1},{2,10},{10,2},{3,11},{11,3},{4,12},{12,4},... | collective-permute-start | bytes 786440 | tf_op jit(solution)/shard_map/ppermute | solution.py:449
  80.5 11.6 %copy-start = (bf16[3,176,384]{2,1,0:T(8,128)(2,1)S(1)}, bf16[3,176,384]{2,1,0:T(8,128)(2,1)}, u32[]{:S(2)}) copy-start(bf16[3,176,384]{2,1,0:T(8,128)(2,1)} %w_out_ref.1) | copy-start | bytes 1216516
  85.4 18.6 %copy-start.1 = (bf16[32,384]{1,0:T(8,128)(2,1)S(1)}, bf16[32,384]{1,0:T(8,128)(2,1)}, u32[]{:S(2)}) copy-start(bf16[32,384]{1,0:T(8,128)(2,1)} %single_ref.1) | copy-start | bytes 73732
  85.4 18.6 %copy-start.2 = (f32[12,32]{1,0:T(8,128)S(1)}, f32[12,32]{1,0:T(8,128)}, u32[]{:S(2)}) copy-start(f32[12,32]{1,0:T(8,128)} %frames_ref.1) | copy-start | bytes 4612
  85.4 18.6 %copy-start.3 = (bf16[384,6]{0,1:T(8,128)(2,1)S(1)}, bf16[384,6]{0,1:T(8,128)(2,1)}, u32[]{:S(2)}) copy-start(bf16[384,6]{0,1:T(8,128)(2,1)} %param.29) | copy-start | bytes 13828
  85.4 18.6 %copy-start.4 = (f32[384]{0:T(512)S(1)}, f32[384]{0:T(512)}, u32[]{:S(2)}) copy-start(f32[384]{0:T(512)} %gain_ref.1) | copy-start | bytes 4612
  88.8 3.4 %collective-permute-start.1 = (f32[128,384]{1,0:T(8,128)S(1)}, f32[128,384]{1,0:T(8,128)S(1)}, u32[]{:S(2)}, u32[]{:S(2)}) collective-permute-start(f32[128,384]{1,0:T(8,128)S(1)} %attend.1.mine_ref), channel_id=1, source_target_pairs={{0,1},{1,0},{2,3},{3,2},{4,5},{5,4},{6,7},{7,6},{8,9},{9,8},{10,11... | collective-permute-start | bytes 589832 | tf_op jit(solution)/shard_map/ppermute | solution.py:471

commit v3 on v2

--- a/solution.py
+++ b/solution.py
@@ -6,7 +6,6 @@
 from jax import lax
 from jax.experimental import pallas as pl
 from jax.experimental.pallas import tpu as pltpu
-from jax.sharding import Mesh
 from jax.sharding import PartitionSpec as P
 
 HIGH = lax.Precision.HIGHEST
@@ -171,7 +170,7 @@
     keys = 2 * far * half
     queries = pair_ref.shape[0]
     width = pair_ref.shape[3]
-    place = lax.axis_index("near")
+    place = lax.axis_index("blk") % 2
     for k in range(far):
         start = pl.multiple_of((2 * k + place) * half, half)
         block[pl.ds(start, half), :] = mine_ref[k]
@@ -344,7 +343,7 @@
     )
 
 
-def spread_kernel(blocks_ref, out_ref):
+def spread_kernel(first, blocks_ref, out_ref):
     blocks, _, wide = blocks_ref.shape
     lines = out_ref.shape[0]
     rows = wide // lines
@@ -362,7 +361,8 @@
             z = jnp.where(g - s == d, up, z)
             z = jnp.where(g - s == d - groups, down, z)
         for q in range(blocks // groups):
-            out_ref[groups * v : groups * (v + 1), HALF * q : HALF * (q + 1)] = z[
+            at = (HALF * q + rows * first) % (rows * blocks)
+            out_ref[groups * v : groups * (v + 1), at : at + HALF] = z[
                 groups * q : groups * (q + 1), :
             ]
 
@@ -444,9 +444,10 @@
         specs=[HBM] * len(inputs),
         name="project",
     )(*(in_hbm(x) for x in inputs))
-    gathered = lax.all_gather(payload, "far", axis=0, tiled=False)
-    swap = [(k, 1 - k) for k in range(2)]
-    across = lax.ppermute(gathered, "near", swap)
+    ways = [list(range(k, blocks, 2)) for k in range(2)]
+    gathered = lax.all_gather(payload, "blk", axis=0, axis_index_groups=ways, tiled=False)
+    swap = [(k, k + 1 - 2 * (k % 2)) for k in range(blocks)]
+    across = lax.ppermute(gathered, "blk", swap)
     bias, pair_here = call(
         functools.partial(bias_kernel, heads),
         (shape((keys, HALF), F32), shape(pair.shape, pair.dtype)),
@@ -468,7 +469,7 @@
         room=24,
         name="attend",
     )(gathered, across, bias, qb, qaux, pair_here)
-    other = lax.ppermute(part, "pair", swap)
+    other = lax.ppermute(part, "pair", [(0, 1), (1, 0)])
     updates = call(
         functools.partial(merge_kernel, heads, size, n_query, n_value),
         shape((lax.axis_size("head"), rows, channels), F32),
@@ -483,21 +484,21 @@
         n=5,
         name="finish",
     )(updates, single, out_gain, w_backbone.T, frames)
-    received = lax.all_to_all(send, ("far", "near"), split_axis=0, concat_axis=0, tiled=True)
+    middle_first = [(k + blocks // 2) % blocks for k in range(blocks)]
+    received = lax.all_to_all(
+        send, "blk", split_axis=0, concat_axis=0, axis_index_groups=[middle_first], tiled=True
+    )
     frames_out = call(
-        spread_kernel, shape((12, blocks * rows), F32), n=1, name="spread"
+        functools.partial(spread_kernel, middle_first[0]),
+        shape((12, blocks * rows), F32),
+        n=1,
+        name="spread",
     )(received)
     return (single_out, frames_out)
 
 
 def solution(mesh):
-    groups, blocks, heads, pairs = (mesh.shape[a] for a in ("groups", "blk", "head", "pair"))
-    near = 2
-    finer = Mesh(
-        mesh.devices.reshape(groups, blocks // near, near, heads, pairs),
-        ("groups", "far", "near", "head", "pair"),
-    )
-    split = ("groups", "far", "near")
+    split = ("groups", "blk")
     placed = (
         P(split, None),
         P(split, None, "pair", None),
@@ -517,7 +518,7 @@
     )
     return jax.shard_map(
         body,
-        mesh=finer,
+        mesh=mesh,
         in_specs=placed,
         out_specs=(P(split, None), P(None, "groups")),
         check_vma=False,

time: 139 us -> 132 us (0.950)
  blocking collectives: 118 us -> 111 us
    all_to_all x1, blocking collectives: 33 us -> 25.9 us  [body(): lax.all_to_all(send, 'blk', split_axis=0, concat_axis=0, axis_index_group...]
  transfers between devices with their start and end apart: 2 -> 2, of which waited for: 1 -> 1; matrix products, arithmetic and copies ran while one was open for 0% -> 0% of each run, Pallas kernels for 3% -> 4%
where the time goes in v3:
time: 132 us
  blocking collectives  111 us (84%)
  Pallas kernels  12.6 us (10%)
  starting transfers between devices  5.66 us (4%)
  waiting for transfers between devices  1.41 us (1%)
    all_gather x1, blocking collectives, body(): lax.all_gather(payload, 'blk', axis=0, axis_index_groups=ways, tiled=False)  74.5 us
    all_to_all x1, blocking collectives, body(): lax.all_to_all(send, 'blk', split_axis=0, concat_axis=0, axis_index_group...  25.9 us
    all_to_all x1, blocking collectives, body(): lax.all_to_all(updates, 'head', split_axis=0, concat_axis=0, tiled=True)  10.8 us
    pallas_call x1, Pallas kernels, body(): call(functools.partial(bias_kernel, heads), (shape((keys, HALF), F32), sh...  4.85 us
    ppermute x1, starting transfers between devices, body(): across = lax.ppermute(gathered, 'blk', swap)  3.71 us
    pallas_call x1, Pallas kernels, body(): call(functools.partial(attend_kernel, n_query), shape((HALF, 3 * HALF), F...  3.31 us
  transfers between devices with their start and end apart: 2, of which 1 were waited for; matrix products, arithmetic and copies ran while one was open for 0% of the time, Pallas kernels for 4%

profile of v3, /device:TPU:40, one launch (start us, length us, event | category | flops | bytes accessed | tf_op | source)
XLA Modules:
  0.0 131.6 jit_solution(8556589458402212966)
XLA Ops:
  0.6 1.7 %project.1 = (f32[16,256]{1,0:T(8,128)S(1)}, f32[128,128]{1,0:T(8,128)S(1)}, f32[16,128]{1,0:T(8,128)S(1)}, f32[128,128]{1,0:T(8,128)S(1)}) custom-call(bf16[32,384]{1,0:T(8,128)(2,1)} %single_ref.1, f32[12,32]{1,0:T(8,128)} %frames_ref.1, s32[32]{0:T(128)} %refs_2_.1, s32[32]{0:T(128)} %refs_3_.1, bf16[48,384]{1,0:T(8,128)(2,1)} %bitcast.12, ...), custom_call_target="tpu_custom_call" | custom-call | tf_op jit(solution)/shard_map/project/pallas_call | solution.py:427
  2.3 74.5 %all-gather = f32[256,256]{1,0:T(8,128)S(1)} all-gather(f32[16,256]{1,0:T(8,128)S(1)} %get-tuple-element.10), channel_id=2, replica_groups={{0,16,32,48,64,80,96,112,128,144,160,176,192,208,224,240},{8,24,40,56,7..., dimensions={0}, use_global_device_ids=true | all-gather | bytes 278528 | tf_op jit(solution)/shard_map/all_gather | solution.py:448
  76.8 3.7 %collective-permute-start = (f32[16,16,256]{2,1,0:T(8,128)S(1)}, f32[16,16,256]{2,1,0:T(8,128)S(1)}, u32[]{:S(2)}, u32[]{:S(2)}) collective-permute-start(f32[16,16,256]{2,1,0:T(8,128)S(1)} %bitcast.7), channel_id=1, source_target_pairs={{0,8},{8,0},{16,24},{24,16},{32,40},{40,32},{48,56},{56,48},{64,72... | collective-permute-start | bytes 786440 | tf_op jit(solution)/shard_map/ppermute | solution.py:450
  80.5 0.0 copy-start
  80.6 4.8 %bias.1 = (f32[512,128]{1,0:T(8,128)S(1)}, bf16[32,32,16,128]{3,2,1,0:T(8,128)(2,1)S(1)}) custom-call(bf16[32,32,16,128]{3,2,1,0:T(8,128)(2,1)} %pair_ref.1, bf16[3,128]{1,0:T(4,128)(2,1)} %bitcast.14), custom_call_target="tpu_custom_call" | custom-call | flops 1000000000 | bytes 4194304 | tf_op jit(solution)/shard_map/bias/pallas_call | solution.py:451
  85.4 0.0 copy-start.1
  85.4 0.0 copy-start.2
  85.4 0.0 copy-start.3
  85.4 0.0 copy-start.4
  85.5 0.0 collective-permute-done.across_ref
  85.5 3.3 %attend.1.mine_ref = f32[128,384]{1,0:T(8,128)S(1)} custom-call(f32[16,16,256]{2,1,0:T(8,128)S(1)} %bitcast.8, f32[16,16,256]{2,1,0:T(8,128)S(1)} %collective-permute-done.across_ref, f32[512,128]{1,0:T(8,128)S(1)} %get-tuple-element.11.bias_ref, f32[128,128]{1,0:T(8,128)S(1)} %get-tuple-element.12.qb_ref, f32[16,128]{1,0:T(8,128)S(1)} %get-tuple-element.13.qaux_ref, ...), custom_call_target="tpu_custom_call" | custom-call | tf_op jit(solution)/shard_map/attend/pallas_call | solution.py:464
  88.8 2.0 %collective-permute-start.1 = (f32[128,384]{1,0:T(8,128)S(1)}, f32[128,384]{1,0:T(8,128)S(1)}, u32[]{:S(2)}, u32[]{:S(2)}) collective-permute-start(f32[128,384]{1,0:T(8,128)S(1)} %attend.1.mine_ref), channel_id=1, source_target_pairs={{0,1},{1,0},{2,3},{3,2},{4,5},{5,4},{6,7},{7,6},{8,9},{9,8},{10,11... | collective-permute-start | bytes 589832 | tf_op jit(solution)/shard_map/ppermute | solution.py:472
  90.7 1.4 %collective-permute-done.1.theirs_ref = f32[128,384]{1,0:T(8,128)S(1)} collective-permute-done((f32[128,384]{1,0:T(8,128)S(1)}, f32[128,384]{1,0:T(8,128)S(1)}, u32[]{:S(2)}, u32[]{:S(2)}) %collective-permute-start.1) | collective-permute-done | bytes 196640 | tf_op jit(solution)/shard_map/ppermute | solution.py:472
  92.2 0.0 copy-done
  92.2 1.1 merge.1
  93.2 10.8 %all_to_all.10.updates_ref = f32[4,32,384]{2,1,0:T(8,128)S(1)} all-to-all(f32[4,32,384]{2,1,0:T(8,128)S(1)} %merge.1), channel_id=1, replica_groups=mesh['groups'=2,'blk'=32,'head'=4,'pair'=2] {'head'}, dimensions={0} | all-to-all | bytes 393216 | tf_op jit(solution)/shard_map/all_to_all | solution.py:480
  104.0 0.0 copy-done.1
  104.0 0.0 copy-done.2
  104.0 0.0 copy-done.3
  104.0 0.0 copy-done.4
  104.0 0.9 finish.1
  104.9 25.9 %all_to_all.11.blocks_ref = f32[32,1,384]{2,1,0:T(1,128)S(1)} all-to-all(f32[32,1,384]{2,1,0:T(1,128)S(1)} %get-tuple-element.17), channel_id=1, replica_groups={{128,136,144,152,160,168,176,184,192,200,208,216,224,232,240,248,0,8,16..., dimensions={0} | all-to-all | bytes 98304 | tf_op jit(solution)/shard_map/all_to_all | solution.py:488
  130.8 0.7 spread.1
Async XLA Ops:
  76.8 8.6 %collective-permute-start = (f32[16,16,256]{2,1,0:T(8,128)S(1)}, f32[16,16,256]{2,1,0:T(8,128)S(1)}, u32[]{:S(2)}, u32[]{:S(2)}) collective-permute-start(f32[16,16,256]{2,1,0:T(8,128)S(1)} %bitcast.7), channel_id=1, source_target_pairs={{0,8},{8,0},{16,24},{24,16},{32,40},{40,32},{48,56},{56,48},{64,72... | collective-permute-start | bytes 786440 | tf_op jit(solution)/shard_map/ppermute | solution.py:450
  80.5 11.6 %copy-start = (bf16[3,176,384]{2,1,0:T(8,128)(2,1)S(1)}, bf16[3,176,384]{2,1,0:T(8,128)(2,1)}, u32[]{:S(2)}) copy-start(bf16[3,176,384]{2,1,0:T(8,128)(2,1)} %w_out_ref.1) | copy-start | bytes 1216516
  85.4 18.6 %copy-start.1 = (bf16[32,384]{1,0:T(8,128)(2,1)S(1)}, bf16[32,384]{1,0:T(8,128)(2,1)}, u32[]{:S(2)}) copy-start(bf16[32,384]{1,0:T(8,128)(2,1)} %single_ref.1) | copy-start | bytes 73732
  85.4 18.6 %copy-start.2 = (f32[12,32]{1,0:T(8,128)S(1)}, f32[12,32]{1,0:T(8,128)}, u32[]{:S(2)}) copy-start(f32[12,32]{1,0:T(8,128)} %frames_ref.1) | copy-start | bytes 4612
  85.4 18.6 %copy-start.3 = (bf16[384,6]{0,1:T(8,128)(2,1)S(1)}, bf16[384,6]{0,1:T(8,128)(2,1)}, u32[]{:S(2)}) copy-start(bf16[384,6]{0,1:T(8,128)(2,1)} %param.29) | copy-start | bytes 13828
  85.4 18.6 %copy-start.4 = (f32[384]{0:T(512)S(1)}, f32[384]{0:T(512)}, u32[]{:S(2)}) copy-start(f32[384]{0:T(512)} %gain_ref.1) | copy-start | bytes 4612
  88.8 3.4 %collective-permute-start.1 = (f32[128,384]{1,0:T(8,128)S(1)}, f32[128,384]{1,0:T(8,128)S(1)}, u32[]{:S(2)}, u32[]{:S(2)}) collective-permute-start(f32[128,384]{1,0:T(8,128)S(1)} %attend.1.mine_ref), channel_id=1, source_target_pairs={{0,1},{1,0},{2,3},{3,2},{4,5},{5,4},{6,7},{7,6},{8,9},{9,8},{10,11... | collective-permute-start | bytes 589832 | tf_op jit(solution)/shard_map/ppermute | solution.py:472

commit v4 on v3

--- a/solution.py
+++ b/solution.py
@@ -16,10 +16,10 @@
 
 SLOTS = 4
 HALF = 128
-BIAS_STEPS = 4
-COMP = 40
-CHAIN, PRESENT, ONE, TOP = 120, 121, 122, 123
+KEYED = 40
+CHAIN, PRESENT, ONE, TOP = 36, 37, 38, 39
 VMEM = pl.BlockSpec(memory_space=pltpu.VMEM)
+SMEM = pl.BlockSpec(memory_space=pltpu.SMEM)
 HBM = pl.BlockSpec(memory_space=pltpu.HBM)
 
 
@@ -45,66 +45,82 @@
     return moved
 
 
-def project_kernel(
-    heads,
-    size,
-    n_query,
-    n_points,
-    *refs,
-):
-    sources, refs = refs[:10], refs[10:]
-    payload_ref, qb_ref, qaux_ref, frows_ref, turned, points, full, spread = refs[:8]
-    local_refs, sem = refs[8:18], refs[18]
+def keys_kernel(heads, size, n_query, n_points, *refs):
+    sources, refs = refs[:6], refs[6:]
+    payload_ref, turned, points, full = refs[:4]
+    local_refs, sem = refs[4:10], refs[10]
     copies = [
         pltpu.make_async_copy(source, target, sem.at[k])
         for k, (source, target) in enumerate(zip(sources, local_refs))
     ]
     for copy in copies:
         copy.start()
-    single_ref, frames_ref, chain_ref, mask_ref, wq_ref, wkv_ref, wqp_ref, wkp_ref = local_refs[:8]
-    hw_ref, cb_ref = local_refs[8:]
+    single_ref, frames_ref, chain_ref, mask_ref, wkv_ref, wkp_ref = local_refs
     full[...] = jnp.zeros_like(full)
     points[...] = jnp.zeros_like(points)
-    spread[...] = jnp.zeros_like(spread)
-    qb_ref[...] = jnp.zeros_like(qb_ref)
-    qaux_ref[...] = jnp.zeros_like(qaux_ref)
     for copy in copies:
         copy.wait()
     rows = single_ref.shape[0]
     half = payload_ref.shape[0]
+    n_value = n_points - n_query
     x = single_ref[...]
-    q_wide = heads * size
-    turned[HALF : HALF + 3 * heads * n_query, :] = dot_nt(wqp_ref[...], x)
-    turned[2 * HALF : 2 * HALF + 3 * heads * n_points, :] = dot_nt(wkp_ref[...], x)
-    full[:, 0 : 2 * q_wide] = dot_nt(x, wkv_ref[...])
-    chain_row = chain_ref[...].astype(F32).reshape(1, rows)
-    mask_row = mask_ref[...].astype(F32).reshape(1, rows)
-
+    turned[...] = dot_nt(wkp_ref[...], x)
+    full[:, 0 : 2 * heads * size] = dot_nt(x, wkv_ref[...])
     count = heads * n_points
-    local = [turned[pl.ds(2 * HALF + b, count, stride=3), :] for b in range(3)]
+    local = [turned[pl.ds(b, count, stride=3), :] for b in range(3)]
     for a, value in enumerate(rotated(frames_ref, local)):
-        points[COMP * a : COMP * a + count, :] = value
-    points[CHAIN : CHAIN + 1, :] = chain_row
-    points[PRESENT : PRESENT + 1, :] = mask_row
+        for h in range(heads):
+            at = heads * n_query * a + n_query * h
+            points[at : at + n_query, :] = value[n_points * h : n_points * h + n_query, :]
+            at = KEYED + heads * n_value * a + n_value * h
+            points[at : at + n_value, :] = value[n_points * h + n_query : n_points * (h + 1), :]
+    points[CHAIN : CHAIN + 1, :] = chain_ref[...].astype(F32).reshape(1, rows)
+    points[PRESENT : PRESENT + 1, :] = mask_ref[...].astype(F32).reshape(1, rows)
     points[ONE : ONE + 1, :] = jnp.ones((1, rows), F32)
     full[:, HALF:] = points[...].T
     start = pl.multiple_of(lax.axis_index("pair") * half, half)
     payload_ref[...] = full[pl.ds(start, half), :]
 
+
+def queries_kernel(
+    heads,
+    size,
+    n_query,
+    single_ref,
+    frames_ref,
+    chain_ref,
+    mask_ref,
+    wq_ref,
+    wqp_ref,
+    hw_ref,
+    cb_ref,
+    qb_ref,
+    qaux_ref,
+    frows_ref,
+    turned,
+    points,
+    spread,
+):
+    rows = single_ref.shape[0]
+    x = single_ref[...]
+    turned[...] = dot_nt(wqp_ref[...], x)
     count = heads * n_query
-    local = [turned[pl.ds(HALF + b, count, stride=3), :] for b in range(3)]
-    spread[0:q_wide, :] = dot_nt(wq_ref[...], x)
+    local = [turned[pl.ds(b, count, stride=3), :] for b in range(3)]
+    spread[...] = jnp.zeros_like(spread)
+    spread[0 : heads * size, :] = dot_nt(wq_ref[...], x)
     for a, value in enumerate(rotated(frames_ref, local)):
         spread[48 + 16 * a : 48 + 16 * a + count, :] = value
-    spread[96:97, :] = chain_row
-    spread[97:98, :] = mask_row
+    spread[96:97, :] = chain_ref[...].astype(F32).reshape(1, rows)
+    spread[97:98, :] = mask_ref[...].astype(F32).reshape(1, rows)
     to_slots = (iota((rows, HALF), 1) // SLOTS == iota((rows, HALF), 0)).astype(F32)
     wide = dot(spread[...], to_slots, HIGH)
     slot = iota((1, HALF), 1) % SLOTS
+    qb_ref[...] = jnp.zeros_like(qb_ref)
     scale = LOGIT_WEIGHT / math.sqrt(size)
     for h in range(heads):
         block = wide[h * size : (h + 1) * size, :] * scale
         qb_ref[2 * size * h : 2 * size * h + size, :] = jnp.where(slot == h, block, 0.0)
+    qaux_ref[...] = jnp.zeros_like(qaux_ref)
     for a in range(3):
         for p in range(n_query):
             line = jnp.zeros((1, HALF), F32)
@@ -123,26 +139,100 @@
     qaux_ref[used + 1 : used + 2, :] = bonus
     qaux_ref[used + 2 : used + 3, :] = wide[96:97, :]
     qaux_ref[used + 3 : used + 4, :] = wide[97:98, :]
-
     points[...] = jnp.zeros_like(points)
     points[0:12, :] = frames_ref[...]
-    columns = points[...].T
     to_rows = (iota((HALF, rows), 0) // SLOTS == iota((HALF, rows), 1)).astype(F32)
-    frows_ref[...] = dot(to_rows, columns, HIGH)
-
-
-def bias_kernel(heads, pair_ref, wb_hbm, bias_ref, here_ref, weights, wb_ref, sem):
-    queries = pair_ref.shape[0]
-    width = pair_ref.shape[3]
-    keys = pair_ref.shape[1] * pair_ref.shape[2]
-    each_step = queries // BIAS_STEPS
-    copies = []
-    for k in range(BIAS_STEPS):
-        part = pl.ds(k * each_step, each_step)
-        copies.append(pltpu.make_async_copy(pair_ref.at[part], here_ref.at[part], sem.at[k]))
-        copies[k].start()
-    small = pltpu.make_async_copy(wb_hbm, wb_ref, sem.at[BIAS_STEPS])
+    frows_ref[...] = dot(to_rows, points[...].T, HIGH)
+
+
+def scores(n_query, block, qb_ref, qaux_ref):
+    keep = iota((block.shape[0], HALF), 1) < KEYED
+    high = jnp.where(keep, block[:, HALF:], 0.0)
+    first = high.astype(BF16).astype(F32)
+    rest = high - first
+    second = rest.astype(BF16).astype(F32)
+    third = (rest - second).astype(BF16).astype(F32)
+    split = first + pltpu.roll(second, KEYED, 1) + pltpu.roll(third, 2 * KEYED, 1)
+    split = split.astype(BF16)
+    row = iota((HALF, HALF), 0)
+    lane = iota((HALF, HALF), 1)
+    slot = lane % SLOTS
+    heads = CHAIN // (3 * n_query)
+    wanted = [
+        jnp.where(slot < heads, n_query * (heads * a + slot) + p, -1)
+        for a in range(3)
+        for p in range(n_query)
+    ]
+    wanted += [jnp.full((HALF, HALF), CHAIN), jnp.full((HALF, HALF), PRESENT)]
+    found = []
+    for k in range(0, len(wanted), 2):
+        picks = [
+            ((row % KEYED == w) & (row < 3 * KEYED)).astype(F32).astype(BF16)
+            for w in wanted[k : k + 2]
+        ]
+        both = dot(split, jnp.concatenate(picks, axis=1))
+        found += [both[:, :HALF], both[:, HALF:]]
+    used = 3 * n_query
+    distance = jnp.zeros((block.shape[0], HALF), F32)
+    for k in range(used):
+        gap = qaux_ref[k : k + 1, :] - found[k]
+        distance += gap * gap
+    scale = qaux_ref[used : used + 1, :]
+    bonus = qaux_ref[used + 1 : used + 2, :]
+    differ = found[used] != qaux_ref[used + 2 : used + 3, :]
+    there = found[used + 1] * qaux_ref[used + 3 : used + 4, :]
+    partial = dot(block[:, :HALF], qb_ref[...], HIGH) + LOGIT_WEIGHT * (
+        jnp.where(differ, bonus, 0.0) - scale * distance
+    )
+    return partial, MASK_PENALTY * (1.0 - there)
+
+
+def softmax_sums(logits, block, turned_w):
+    by_row = logits.T
+    top = jnp.max(by_row, axis=1, keepdims=True)
+    weights = jnp.exp(by_row - top)
+    turned_w[...] = weights
+    return top, dot(weights, block, HIGH)
+
+
+def side(pair_ref, i, parity):
+    _, far, _, half, width = pair_ref.shape
+    return pair_ref[i, :, parity].reshape(far * half, width)
+
+
+def pair_sums(turned_w, pair_ref, parity, g):
+    width = pair_ref.shape[4]
+    rows = slice(2 * SLOTS * g, 2 * SLOTS * (g + 1))
+    right = jnp.concatenate(
+        [side(pair_ref, 2 * g, parity), side(pair_ref, 2 * g + 1, parity)], axis=1
+    )
+    both = dot(turned_w[rows, :].astype(BF16), right)
+    upper = iota((2 * SLOTS, width), 0) < SLOTS
+    return rows, jnp.where(upper, both[:, :width], both[:, width:])
+
+
+def near_kernel(
+    heads,
+    n_query,
+    pair_ref,
+    wb_hbm,
+    mine_ref,
+    qb_ref,
+    qaux_ref,
+    part_ref,
+    bias_ref,
+    weights,
+    turned_w,
+    wb_ref,
+    sem,
+):
+    queries, far, _, half, width = pair_ref.shape
+    keys = far * half
+    place = lax.axis_index("blk") % 2
+    small = pltpu.make_async_copy(wb_hbm, wb_ref, sem)
     small.start()
+    block = mine_ref[...].reshape(keys, mine_ref.shape[2])
+    partial, penalty = scores(n_query, block, qb_ref, qaux_ref)
     lane = iota((width, HALF), 1)
     row = iota((HALF, width), 0)
     small.wait()
@@ -155,79 +245,43 @@
         weights[i * width : (i + 1) * width, :] = jnp.where(
             lane // SLOTS == i, each, 0.0
         ).astype(BF16)
-    for k in range(BIAS_STEPS):
-        copies[k].wait()
-        these = range(k * each_step, (k + 1) * each_step)
-        left = jnp.concatenate([here_ref[i].reshape(keys, width) for i in these], axis=1)
-        found = dot(left, weights[these[0] * width : (these[-1] + 1) * width, :])
-        bias_ref[...] = found if k == 0 else bias_ref[...] + found
-
-
-def attend_kernel(
-    n_query, mine_ref, across_ref, bias_ref, qb_ref, qaux_ref, pair_ref, part_ref, turned_w, block
+
+    def bias_of(parity):
+        left = jnp.concatenate([side(pair_ref, i, parity) for i in range(queries)], axis=1)
+        return dot(left, weights[...])
+
+    logits = (partial + LOGIT_WEIGHT * bias_of(place)) - penalty
+    top, sums = softmax_sums(logits, block, turned_w)
+    part_ref[:, HALF:] = jnp.where(iota(sums.shape, 1) == HALF + TOP, top, sums)
+    for g in range(queries // 2):
+        rows, found = pair_sums(turned_w, pair_ref, place, g)
+        part_ref[rows, 0:width] = found
+    bias_ref[...] = bias_of(1 - place)
+
+
+def across_kernel(
+    n_query, part_in, across_ref, bias_ref, qb_ref, qaux_ref, pair_ref, part_ref, turned_w
 ):
-    far, half, lanes = mine_ref.shape
-    keys = 2 * far * half
-    queries = pair_ref.shape[0]
-    width = pair_ref.shape[3]
+    far, half, lanes = across_ref.shape
+    width = pair_ref.shape[4]
     place = lax.axis_index("blk") % 2
-    for k in range(far):
-        start = pl.multiple_of((2 * k + place) * half, half)
-        block[pl.ds(start, half), :] = mine_ref[k]
-        start = pl.multiple_of((2 * k + 1 - place) * half, half)
-        block[pl.ds(start, half), :] = across_ref[k]
-    high = block[:, HALF:]
-    first = high.astype(BF16)
-    rest = high - first.astype(F32)
-    second = rest.astype(BF16)
-    third = (rest - second.astype(F32)).astype(BF16)
-    split = jnp.concatenate([first, second, third], axis=1)
-
-    row = iota((HALF, HALF), 0)
-    lane = iota((HALF, HALF), 1)
-    slot = lane % SLOTS
-
-    def expanded(wanted):
-        picks = (row == wanted).astype(F32).astype(BF16)
-        return dot(split, jnp.concatenate([picks, picks, picks], axis=0))
-
-    distance = jnp.zeros((keys, HALF), F32)
-    for a in range(3):
-        for p in range(n_query):
-            wanted = jnp.where(slot < 3, COMP * a + 12 * slot + p, -1)
-            at = n_query * a + p
-            gap = qaux_ref[at : at + 1, :] - expanded(wanted)
-            distance += gap * gap
-    used = 3 * n_query
-    scale = qaux_ref[used : used + 1, :]
-    bonus = qaux_ref[used + 1 : used + 2, :]
-    differ = expanded(jnp.full((HALF, HALF), CHAIN)) != qaux_ref[used + 2 : used + 3, :]
-    there = expanded(jnp.full((HALF, HALF), PRESENT)) * qaux_ref[used + 3 : used + 4, :]
-    logits = dot(block[:, :HALF], qb_ref[...], HIGH) + LOGIT_WEIGHT * (
-        bias_ref[...] - scale * distance + jnp.where(differ, bonus, 0.0)
-    )
-    logits = logits - MASK_PENALTY * (1.0 - there)
-    by_row = logits.T
-    top = jnp.max(by_row, axis=1, keepdims=True)
-    weights = jnp.exp(by_row - top)
-    turned_w[...] = weights
-    sums = dot(weights, block[...], HIGH)
-    part_ref[:, HALF:] = jnp.where(iota((HALF, lanes), 1) == HALF + TOP, top, sums)
-    upper = iota((2 * SLOTS, width), 0) < SLOTS
-    for g in range(queries // 2):
-        rows = slice(2 * SLOTS * g, 2 * SLOTS * (g + 1))
-        right = jnp.concatenate(
-            [pair_ref[2 * g].reshape(keys, width), pair_ref[2 * g + 1].reshape(keys, width)],
-            axis=1,
-        )
-        both = dot(turned_w[rows, :].astype(BF16), right)
-        part_ref[rows, 0:width] = jnp.where(upper, both[:, :width], both[:, width:])
+    block = across_ref[...].reshape(far * half, lanes)
+    partial, penalty = scores(n_query, block, qb_ref, qaux_ref)
+    logits = (partial + LOGIT_WEIGHT * bias_ref[...]) - penalty
+    top, sums = softmax_sums(logits, block, turned_w)
+    before = part_in[:, 2 * HALF + TOP : 2 * HALF + TOP + 1]
+    best = jnp.maximum(before, top)
+    old, new = jnp.exp(before - best), jnp.exp(top - best)
+    merged = part_in[:, HALF:] * old + sums * new
+    part_ref[:, HALF:] = jnp.where(iota(sums.shape, 1) == HALF + TOP, best, merged)
+    for g in range(pair_ref.shape[0] // 2):
+        rows, found = pair_sums(turned_w, pair_ref, 1 - place, g)
+        part_ref[rows, 0:width] = part_in[rows, 0:width] * old[rows, :] + found * new[rows, :]
 
 
 def merge_kernel(
     heads,
     size,
-    n_query,
     n_value,
     mine_ref,
     theirs_ref,
@@ -254,9 +308,8 @@
         return picked
 
     attended = of_own_head(HALF + size, 2 * size, size)
-    n_points = n_query + n_value
     moved = [
-        of_own_head(2 * HALF + COMP * a + n_query, n_points, n_value)
+        of_own_head(2 * HALF + KEYED + heads * n_value * a, n_value, n_value)
         - frows_ref[:, 9 + a : 10 + a]
         for a in range(3)
     ]
@@ -412,66 +465,63 @@
     keys = blocks * half
     shape = jax.ShapeDtypeStruct
 
-    inputs = (
-        single,
-        frames,
-        chain,
-        mask,
-        w_query.T,
-        w_key_value.T,
-        w_query_points.T,
-        w_kv_points.T,
-        head_weights,
-        chain_bias,
-    )
-    payload, qb, qaux, frows = call(
-        functools.partial(project_kernel, heads, size, n_query, n_points),
+    inputs = (single, frames, chain, mask, w_key_value.T, w_kv_points.T)
+    payload = call(
+        functools.partial(keys_kernel, heads, size, n_query, n_points),
+        shape((half, 2 * HALF), F32),
         (
-            shape((half, 2 * HALF), F32),
-            shape((HALF, HALF), F32),
-            shape((16, HALF), F32),
-            shape((HALF, HALF), F32),
-        ),
-        (
-            pltpu.VMEM((3 * HALF, rows), F32),
+            pltpu.VMEM((3 * heads * n_points, rows), F32),
             pltpu.VMEM((HALF, rows), F32),
             pltpu.VMEM((rows, 2 * HALF), F32),
-            pltpu.VMEM((104, rows), F32),
-            *(pltpu.VMEM(x.shape, x.dtype) for x in inputs[:8]),
-            *(pltpu.SMEM(x.shape, x.dtype) for x in inputs[8:]),
+            *(pltpu.VMEM(x.shape, x.dtype) for x in inputs),
             pltpu.SemaphoreType.DMA((len(inputs),)),
         ),
         specs=[HBM] * len(inputs),
-        name="project",
+        cost=pl.CostEstimate(flops=10**10, bytes_accessed=4 * pair.size, transcendentals=0),
+        name="keys",
     )(*(in_hbm(x) for x in inputs))
     ways = [list(range(k, blocks, 2)) for k in range(2)]
     gathered = lax.all_gather(payload, "blk", axis=0, axis_index_groups=ways, tiled=False)
     swap = [(k, k + 1 - 2 * (k % 2)) for k in range(blocks)]
     across = lax.ppermute(gathered, "blk", swap)
-    bias, pair_here = call(
-        functools.partial(bias_kernel, heads),
-        (shape((keys, HALF), F32), shape(pair.shape, pair.dtype)),
+    qb, qaux, frows = call(
+        functools.partial(queries_kernel, heads, size, n_query),
+        (shape((HALF, HALF), F32), shape((16, HALF), F32), shape((HALF, HALF), F32)),
+        (
+            pltpu.VMEM((3 * heads * n_query, rows), F32),
+            pltpu.VMEM((HALF, rows), F32),
+            pltpu.VMEM((104, rows), F32),
+        ),
+        specs=[VMEM] * 6 + [SMEM] * 2,
+        cost=pl.CostEstimate(flops=10**8, bytes_accessed=10**5, transcendentals=0),
+        name="queries",
+    )(single, frames, chain, mask, w_query.T, w_query_points.T, head_weights, chain_bias)
+    halves = pair.reshape(rows, blocks // 2, 2, half, width)
+    part, bias = call(
+        functools.partial(near_kernel, heads, n_query),
+        (shape((HALF, 3 * HALF), F32), shape((keys // 2, HALF), F32)),
         (
             pltpu.VMEM((rows * width, HALF), BF16),
+            pltpu.VMEM((HALF, keys // 2), F32),
             pltpu.VMEM((heads, width), w_pair_bias.dtype),
-            pltpu.SemaphoreType.DMA((BIAS_STEPS + 1,)),
+            pltpu.SemaphoreType.DMA,
         ),
-        specs=[HBM, HBM],
+        specs=[VMEM, HBM, VMEM, VMEM, VMEM],
         room=16,
         cost=pl.CostEstimate(flops=10**9, bytes_accessed=2 * pair.size, transcendentals=0),
-        name="bias",
-    )(in_hbm(pair), in_hbm(w_pair_bias.T))
+        name="near",
+    )(halves, in_hbm(w_pair_bias.T), gathered, qb, qaux)
     part = call(
-        functools.partial(attend_kernel, n_query),
+        functools.partial(across_kernel, n_query),
         shape((HALF, 3 * HALF), F32),
-        (pltpu.VMEM((HALF, keys), F32), pltpu.VMEM((keys, 2 * HALF), F32)),
+        (pltpu.VMEM((HALF, keys // 2), F32),),
         n=6,
-        room=24,
-        name="attend",
-    )(gathered, across, bias, qb, qaux, pair_here)
+        room=16,
+        name="across",
+    )(part, across, bias, qb, qaux, halves)
     other = lax.ppermute(part, "pair", [(0, 1), (1, 0)])
     updates = call(
-        functools.partial(merge_kernel, heads, size, n_query, n_value),
+        functools.partial(merge_kernel, heads, size, n_value),
         shape((lax.axis_size("head"), rows, channels), F32),
         (pltpu.VMEM((HALF, HALF), F32), pltpu.VMEM((HALF, HALF), F32)),
         n=4,

time: 132 us -> 130 us (0.985)
  Pallas kernels: 12.6 us -> 9.42 us
    pallas_call x4 -> x5, Pallas kernels: 10.9 us -> 7.75 us  [the longest x1 2.85 us: body(): call(functools.partial(near_kernel, heads, n_query), (shape((HALF, 3 * HA...]
  transfers between devices with their start and end apart: 2 -> 2, of which waited for: 1 -> 2; matrix products, arithmetic and copies ran while one was open for 0% -> 0% of each run, Pallas kernels for 4% -> 3%
where the time goes in v4:
time: 130 us; the launch traced here: 129 us
  blocking collectives  111 us (85%)
  Pallas kernels  9.42 us (7%)
  starting transfers between devices  5.57 us (4%)
  waiting for transfers between devices  2.05 us (2%)
    all_gather x1, blocking collectives, body(): lax.all_gather(payload, 'blk', axis=0, axis_index_groups=ways, tiled=False)  74.3 us
    all_to_all x1, blocking collectives, body(): lax.all_to_all(send, 'blk', split_axis=0, concat_axis=0, axis_index_group...  26.2 us
    all_to_all x1, blocking collectives, body(): lax.all_to_all(updates, 'head', split_axis=0, concat_axis=0, tiled=True)  10.8 us
    ppermute x1, starting transfers between devices, body(): across = lax.ppermute(gathered, 'blk', swap)  3.61 us
    pallas_call x1, Pallas kernels, body(): call(functools.partial(near_kernel, heads, n_query), (shape((HALF, 3 * HA...  2.85 us
  transfers between devices with their start and end apart: 2, of which 2 were waited for; matrix products, arithmetic and copies ran while one was open for 0% of the time, Pallas kernels for 3%

profile of v4, /device:TPU:40, one launch (start us, length us, event | category | flops | bytes accessed | tf_op | source)
XLA Modules:
  0.0 129.3 jit_solution(17000596709688897534)
XLA Ops:
  0.6 0.0 copy-start.2
  0.6 0.0 copy-start.3
  0.7 0.0 copy-start.6
  0.7 0.0 copy-start.7
  0.7 0.0 copy-start.8
  0.7 0.0 copy-start.9
  0.7 0.0 copy-start.10
  0.7 0.0 copy-start.11
  0.7 0.0 copy-start
  0.7 1.5 %keys.1 = f32[16,256]{1,0:T(8,128)S(1)} custom-call(bf16[32,384]{1,0:T(8,128)(2,1)} %single_ref.3, f32[12,32]{1,0:T(8,128)} %frames_ref.3, s32[32]{0:T(128)} %chain_ref.1, s32[32]{0:T(128)} %mask_ref.1, bf16[96,384]{1,0:T(8,128)(2,1)} %bitcast.17, bf16[108,384]{1,0:T(8,128)(2,1)} %bitcast.16), custom_call_target="tpu_custom_call" | custom-call | flops 10000000000 | bytes 8388608 | tf_op jit(solution)/shard_map/keys/pallas_call | solution.py:469
  2.2 74.3 %all-gather = f32[256,256]{1,0:T(8,128)S(1)} all-gather(f32[16,256]{1,0:T(8,128)S(1)} %keys.1), channel_id=2, replica_groups={{0,16,32,48,64,80,96,112,128,144,160,176,192,208,224,240},{8,24,40,56,7..., dimensions={0}, use_global_device_ids=true | all-gather | bytes 278528 | tf_op jit(solution)/shard_map/all_gather | solution.py:484
  76.5 3.6 %collective-permute-start = (f32[16,16,256]{2,1,0:T(8,128)S(1)}, f32[16,16,256]{2,1,0:T(8,128)S(1)}, u32[]{:S(2)}, u32[]{:S(2)}) collective-permute-start(f32[16,16,256]{2,1,0:T(8,128)S(1)} %bitcast.10), channel_id=1, source_target_pairs={{0,8},{8,0},{16,24},{24,16},{32,40},{40,32},{48,56},{56,48},{64,72... | collective-permute-start | bytes 786440 | tf_op jit(solution)/shard_map/ppermute | solution.py:486
  80.1 0.0 copy-done.2
  80.1 0.0 copy-done.3
  80.1 0.0 copy-done.6
  80.1 0.0 copy-done.7
  80.2 0.0 copy-done.8
  80.2 0.0 copy-done.9
  80.2 0.0 copy-done.10
  80.2 0.0 copy-done.11
  80.2 1.0 queries.1
  81.2 0.0 copy-done
  81.2 0.0 copy-start.1
  81.3 2.9 %near.1 = (f32[128,384]{1,0:T(8,128)S(1)}, f32[256,128]{1,0:T(8,128)S(1)}) custom-call(bf16[32,16,2,16,128]{4,3,2,1,0:T(8,128)(2,1)S(1)} %bitcast.8, bf16[3,128]{1,0:T(4,128)(2,1)} %bitcast.15, f32[16,16,256]{2,1,0:T(8,128)S(1)} %bitcast.11, f32[128,128]{1,0:T(8,128)S(1)} %get-tuple-element.9.qb_ref, f32[16,128]{1,0:T(8,128)S(1)} %get-tuple-element.10.qaux_ref), custom_call_target="tpu_custom_call" | custom-call | flops 1000000000 | bytes 4194304 | tf_op jit(solution)/shard_map/near/pallas_call | solution.py:500
  84.1 0.0 copy-start.4
  84.1 0.0 copy-start.5
  84.1 0.6 collective-permute-done.across_ref
  84.8 1.3 %across.1.mine_ref = f32[128,384]{1,0:T(8,128)S(1)} custom-call(f32[128,384]{1,0:T(8,128)S(1)} %get-tuple-element.11.part_in, f32[16,16,256]{2,1,0:T(8,128)S(1)} %collective-permute-done.across_ref, f32[256,128]{1,0:T(8,128)S(1)} %get-tuple-element.12.bias_ref, f32[128,128]{1,0:T(8,128)S(1)} %get-tuple-element.9.qb_ref, ...), custom_call_target="tpu_custom_call" | custom-call | tf_op jit(solution)/shard_map/across/pallas_call | solution.py:514
  86.1 2.0 %collective-permute-start.1 = (f32[128,384]{1,0:T(8,128)S(1)}, f32[128,384]{1,0:T(8,128)S(1)}, u32[]{:S(2)}, u32[]{:S(2)}) collective-permute-start(f32[128,384]{1,0:T(8,128)S(1)} %across.1.mine_ref), channel_id=1, source_target_pairs={{0,1},{1,0},{2,3},{3,2},{4,5},{5,4},{6,7},{7,6},{8,9},{9,8},{10,11... | collective-permute-start | bytes 589832 | tf_op jit(solution)/shard_map/ppermute | solution.py:522
  88.1 1.4 %collective-permute-done.1.theirs_ref = f32[128,384]{1,0:T(8,128)S(1)} collective-permute-done((f32[128,384]{1,0:T(8,128)S(1)}, f32[128,384]{1,0:T(8,128)S(1)}, u32[]{:S(2)}, u32[]{:S(2)}) %collective-permute-start.1) | collective-permute-done | bytes 196640 | tf_op jit(solution)/shard_map/ppermute | solution.py:522
  89.5 0.0 copy-done.1
  89.5 1.1 merge.1
  90.6 10.8 %all_to_all.10.updates_ref = f32[4,32,384]{2,1,0:T(8,128)S(1)} all-to-all(f32[4,32,384]{2,1,0:T(8,128)S(1)} %merge.1), channel_id=1, replica_groups=mesh['groups'=2,'blk'=32,'head'=4,'pair'=2] {'head'}, dimensions={0} | all-to-all | bytes 393216 | tf_op jit(solution)/shard_map/all_to_all | solution.py:530
  101.4 0.0 copy-done.4
  101.4 0.0 copy-done.5
  101.4 0.9 finish.1
  102.3 26.2 %all_to_all.11.blocks_ref = f32[32,1,384]{2,1,0:T(1,128)S(1)} all-to-all(f32[32,1,384]{2,1,0:T(1,128)S(1)} %get-tuple-element.15), channel_id=1, replica_groups={{128,136,144,152,160,168,176,184,192,200,208,216,224,232,240,248,0,8,16..., dimensions={0} | all-to-all | bytes 98304 | tf_op jit(solution)/shard_map/all_to_all | solution.py:538
  128.6 0.7 spread.1
Async XLA Ops:
  0.6 79.5 %copy-start.2 = (bf16[32,384]{1,0:T(8,128)(2,1)S(1)}, bf16[32,384]{1,0:T(8,128)(2,1)}, u32[]{:S(2)}) copy-start(bf16[32,384]{1,0:T(8,128)(2,1)} %single_ref.3) | copy-start | bytes 73732
  0.6 79.5 %copy-start.3 = (f32[12,32]{1,0:T(8,128)S(1)}, f32[12,32]{1,0:T(8,128)}, u32[]{:S(2)}) copy-start(f32[12,32]{1,0:T(8,128)} %frames_ref.3) | copy-start | bytes 4612
  0.7 79.5 %copy-start.6 = (bf16[384,48]{0,1:T(8,128)(2,1)S(1)}, bf16[384,48]{0,1:T(8,128)(2,1)}, u32[]{:S(2)}) copy-start(bf16[384,48]{0,1:T(8,128)(2,1)} %param.20) | copy-start | bytes 110596
  0.7 79.5 %copy-start.7 = (bf16[384,36]{0,1:T(8,128)(2,1)S(1)}, bf16[384,36]{0,1:T(8,128)(2,1)}, u32[]{:S(2)}) copy-start(bf16[384,36]{0,1:T(8,128)(2,1)} %param.22) | copy-start | bytes 82948
  0.7 79.5 %copy-start.8 = (s32[32]{0:T(128)S(1)}, s32[32]{0:T(128)}, u32[]{:S(2)}) copy-start(s32[32]{0:T(128)} %chain_ref.1) | copy-start | bytes 388
  0.7 79.5 %copy-start.9 = (s32[32]{0:T(128)S(1)}, s32[32]{0:T(128)}, u32[]{:S(2)}) copy-start(s32[32]{0:T(128)} %mask_ref.1) | copy-start | bytes 388
  0.7 79.5 %copy-start.10 = (f32[3]{0:T(128)S(1)}, f32[3]{0:T(128)}, u32[]{:S(2)}) copy-start(f32[3]{0:T(128)} %hw_ref.1) | copy-start | bytes 40
  0.7 79.5 %copy-start.11 = (f32[3]{0:T(128)S(1)}, f32[3]{0:T(128)}, u32[]{:S(2)}) copy-start(f32[3]{0:T(128)} %cb_ref.1) | copy-start | bytes 40
  0.7 80.5 %copy-start = (bf16[32,32,16,128]{3,2,1,0:T(8,128)(2,1)S(1)}, bf16[32,32,16,128]{3,2,1,0:T(8,128)(2,1)}, u32[]{:S(2)}) copy-start(bf16[32,32,16,128]{3,2,1,0:T(8,128)(2,1)} %param.16) | copy-start | bytes 12582916
  76.5 8.3 %collective-permute-start = (f32[16,16,256]{2,1,0:T(8,128)S(1)}, f32[16,16,256]{2,1,0:T(8,128)S(1)}, u32[]{:S(2)}, u32[]{:S(2)}) collective-permute-start(f32[16,16,256]{2,1,0:T(8,128)S(1)} %bitcast.10), channel_id=1, source_target_pairs={{0,8},{8,0},{16,24},{24,16},{32,40},{40,32},{48,56},{56,48},{64,72... | collective-permute-start | bytes 786440 | tf_op jit(solution)/shard_map/ppermute | solution.py:486
  81.2 8.3 %copy-start.1 = (bf16[3,176,384]{2,1,0:T(8,128)(2,1)S(1)}, bf16[3,176,384]{2,1,0:T(8,128)(2,1)}, u32[]{:S(2)}) copy-start(bf16[3,176,384]{2,1,0:T(8,128)(2,1)} %w_out_ref.1) | copy-start | bytes 1216516
  84.1 17.3 %copy-start.4 = (bf16[384,6]{0,1:T(8,128)(2,1)S(1)}, bf16[384,6]{0,1:T(8,128)(2,1)}, u32[]{:S(2)}) copy-start(bf16[384,6]{0,1:T(8,128)(2,1)} %param.29) | copy-start | bytes 13828
  84.1 17.3 %copy-start.5 = (f32[384]{0:T(512)S(1)}, f32[384]{0:T(512)}, u32[]{:S(2)}) copy-start(f32[384]{0:T(512)} %gain_ref.1) | copy-start | bytes 4612
  86.1 3.4 %collective-permute-start.1 = (f32[128,384]{1,0:T(8,128)S(1)}, f32[128,384]{1,0:T(8,128)S(1)}, u32[]{:S(2)}, u32[]{:S(2)}) collective-permute-start(f32[128,384]{1,0:T(8,128)S(1)} %across.1.mine_ref), channel_id=1, source_target_pairs={{0,1},{1,0},{2,3},{3,2},{4,5},{5,4},{6,7},{7,6},{8,9},{9,8},{10,11... | collective-permute-start | bytes 589832 | tf_op jit(solution)/shard_map/ppermute | solution.py:522

commit v5 on v4

--- a/solution.py
+++ b/solution.py
@@ -47,8 +47,8 @@
 
 def keys_kernel(heads, size, n_query, n_points, *refs):
     sources, refs = refs[:6], refs[6:]
-    payload_ref, turned, points, full = refs[:4]
-    local_refs, sem = refs[4:10], refs[10]
+    payload_ref, turned, points, full, spare = refs[:5]
+    local_refs, sem = refs[5:11], refs[11]
     copies = [
         pltpu.make_async_copy(source, target, sem.at[k])
         for k, (source, target) in enumerate(zip(sources, local_refs))
@@ -56,7 +56,7 @@
     for copy in copies:
         copy.start()
     single_ref, frames_ref, chain_ref, mask_ref, wkv_ref, wkp_ref = local_refs
-    full[...] = jnp.zeros_like(full)
+    spare[...] = jnp.zeros_like(spare)
     points[...] = jnp.zeros_like(points)
     for copy in copies:
         copy.wait()
@@ -65,7 +65,12 @@
     n_value = n_points - n_query
     x = single_ref[...]
     turned[...] = dot_nt(wkp_ref[...], x)
-    full[:, 0 : 2 * heads * size] = dot_nt(x, wkv_ref[...])
+    edge = 2 * heads * size
+    values = frames_ref[...]
+    spare[edge : edge + 12, :] = values
+    spare[edge + 12 : edge + 24, :] = jnp.concatenate([values[:, half:], values[:, :half]], axis=1)
+    full[:, :HALF] = spare[...].T
+    full[:, 0:edge] = dot_nt(x, wkv_ref[...])
     count = heads * n_points
     local = [turned[pl.ds(b, count, stride=3), :] for b in range(3)]
     for a, value in enumerate(rotated(frames_ref, local)):
@@ -287,6 +292,7 @@
     theirs_ref,
     frows_ref,
     w_out_ref,
+    _,
     out_ref,
     small,
     large,
@@ -348,7 +354,7 @@
         out_ref[k] = update
 
 
-def finish_kernel(updates_ref, single_ref, gain_ref, wb_ref, frames_ref, out_ref, send_ref):
+def finish_kernel(updates_ref, single_ref, gain_ref, wb_ref, out_ref, send_ref):
     copies, rows, channels = updates_ref.shape
     mixed = single_ref[...].astype(F32)
     update = updates_ref[0]
@@ -362,29 +368,12 @@
     single_out = (away * lax.rsqrt(spread + 1e-05) * gain).astype(BF16)
     out_ref[...] = single_out
     motion = dot_nt(wb_ref[...], single_out)
-    m = [motion[k : k + 1, :] for k in range(6)]
-    qa = 1.0 / jnp.sqrt(1.0 + m[0] * m[0] + m[1] * m[1] + m[2] * m[2])
-    qb, qc, qd = m[0] * qa, m[1] * qa, m[2] * qa
-    spin = [
-        [qa * qa + qb * qb - qc * qc - qd * qd, 2.0 * (qb * qc - qa * qd), 2.0 * (qb * qd + qa * qc)],
-        [2.0 * (qb * qc + qa * qd), qa * qa - qb * qb + qc * qc - qd * qd, 2.0 * (qc * qd - qa * qb)],
-        [2.0 * (qb * qd - qa * qc), 2.0 * (qc * qd + qa * qb), qa * qa - qb * qb - qc * qc + qd * qd],
-    ]
-    r = [[frames_ref[3 * a + b : 3 * a + b + 1, :] for b in range(3)] for a in range(3)]
-    lines = []
-    for a in range(3):
-        for c in range(3):
-            lines.append(r[a][0] * spin[0][c] + r[a][1] * spin[1][c] + r[a][2] * spin[2][c])
-    for a in range(3):
-        lines.append(
-            frames_ref[9 + a : 10 + a, :] + (r[a][0] * m[3] + r[a][1] * m[4] + r[a][2] * m[5])
-        )
     groups = HALF // rows
     repeat = (iota((rows, HALF), 1) % rows == iota((rows, HALF), 0)).astype(F32)
-    wide = dot(jnp.concatenate(lines + lines[:4], axis=0), repeat, HIGH)
+    wide = dot(jnp.concatenate([motion, motion[:2]], axis=0), repeat, HIGH)
     group = iota((1, HALF), 1) // rows
     pieces = []
-    for v in range(len(lines) // groups):
+    for v in range(wide.shape[0] // groups):
         piece = wide[groups * v : groups * v + 1, :]
         for s in range(1, groups):
             at = groups * v + s
@@ -396,10 +385,28 @@
     )
 
 
-def spread_kernel(first, blocks_ref, out_ref):
+def frames_kernel(edge, mine_ref, across_ref, out_ref, order):
+    far, half, _ = mine_ref.shape
+    place = lax.axis_index("blk") % 2
+    which = lax.axis_index("pair")
+    for ref, parity in ((mine_ref, place), (across_ref, 1 - place)):
+        x = ref[:, :, :HALF].reshape(far * half, HALF)
+        own = pltpu.roll(x, HALF - edge, 1)
+        other = pltpu.roll(x, HALF - edge - 12, 1)
+        for k in range(far):
+            base = (2 * k + parity) * 2 * half
+            rows = slice(k * half, (k + 1) * half)
+            order[pl.ds(pl.multiple_of(base + which * half, half), half), :] = own[rows, :]
+            order[pl.ds(pl.multiple_of(base + (1 - which) * half, half), half), :] = other[rows, :]
+    for q in range(4 * far * half // HALF):
+        at = slice(HALF * q, HALF * (q + 1))
+        out_ref[:, at] = order[at, :].T[0:12, :]
+
+
+def spread_kernel(first, blocks_ref, frames_ref, single_ref, out_ref, single_out_ref, motion):
+    single_out_ref[...] = single_ref[...]
     blocks, _, wide = blocks_ref.shape
-    lines = out_ref.shape[0]
-    rows = wide // lines
+    rows = frames_ref.shape[1] // blocks
     groups = HALF // rows
     x = blocks_ref[...].reshape(blocks, wide)
     s = iota((blocks, HALF), 0) % groups
@@ -415,9 +422,24 @@
             z = jnp.where(g - s == d - groups, down, z)
         for q in range(blocks // groups):
             at = (HALF * q + rows * first) % (rows * blocks)
-            out_ref[groups * v : groups * (v + 1), at : at + HALF] = z[
+            motion[groups * v : groups * (v + 1), at : at + HALF] = z[
                 groups * q : groups * (q + 1), :
             ]
+    m = [motion[k : k + 1, :] for k in range(6)]
+    qa = 1.0 / jnp.sqrt(1.0 + m[0] * m[0] + m[1] * m[1] + m[2] * m[2])
+    qb, qc, qd = m[0] * qa, m[1] * qa, m[2] * qa
+    spin = [
+        [qa * qa + qb * qb - qc * qc - qd * qd, 2.0 * (qb * qc - qa * qd), 2.0 * (qb * qd + qa * qc)],
+        [2.0 * (qb * qc + qa * qd), qa * qa - qb * qb + qc * qc - qd * qd, 2.0 * (qc * qd - qa * qb)],
+        [2.0 * (qb * qd - qa * qc), 2.0 * (qc * qd + qa * qb), qa * qa - qb * qb - qc * qc + qd * qd],
+    ]
+    for a in range(3):
+        r = [frames_ref[3 * a + b : 3 * a + b + 1, :] for b in range(3)]
+        for c in range(3):
+            line = r[0] * spin[0][c] + r[1] * spin[1][c] + r[2] * spin[2][c]
+            out_ref[3 * a + c : 3 * a + c + 1, :] = line
+        moved = r[0] * m[3] + r[1] * m[4] + r[2] * m[5]
+        out_ref[9 + a : 10 + a, :] = frames_ref[9 + a : 10 + a, :] + moved
 
 
 def in_hbm(x):
@@ -473,6 +495,7 @@
             pltpu.VMEM((3 * heads * n_points, rows), F32),
             pltpu.VMEM((HALF, rows), F32),
             pltpu.VMEM((rows, 2 * HALF), F32),
+            pltpu.VMEM((HALF, rows), F32),
             *(pltpu.VMEM(x.shape, x.dtype) for x in inputs),
             pltpu.SemaphoreType.DMA((len(inputs),)),
         ),
@@ -520,30 +543,43 @@
         name="across",
     )(part, across, bias, qb, qaux, halves)
     other = lax.ppermute(part, "pair", [(0, 1), (1, 0)])
+    all_frames = call(
+        functools.partial(frames_kernel, 2 * heads * size),
+        shape((12, blocks * rows), F32),
+        (pltpu.VMEM((blocks * rows, HALF), F32),),
+        n=2,
+        cost=pl.CostEstimate(flops=10**8, bytes_accessed=10**6, transcendentals=0),
+        name="frames",
+    )(gathered, across)
     updates = call(
         functools.partial(merge_kernel, heads, size, n_value),
         shape((lax.axis_size("head"), rows, channels), F32),
         (pltpu.VMEM((HALF, HALF), F32), pltpu.VMEM((HALF, HALF), F32)),
+        n=5,
+        name="merge",
+    )(part, other, frows, w_out, all_frames)
+    sides = lax.axis_size("head")
+    last_first = [(k + sides - 1) % sides for k in range(sides)]
+    updates = lax.all_to_all(
+        updates, "head", split_axis=0, concat_axis=0, axis_index_groups=[last_first], tiled=True
+    )
+    single_here, send = call(
+        finish_kernel,
+        (shape((rows, channels), BF16), shape((blocks, 1, 8 * rows), F32)),
         n=4,
-        name="merge",
-    )(part, other, frows, w_out)
-    updates = lax.all_to_all(updates, "head", split_axis=0, concat_axis=0, tiled=True)
-    single_out, send = call(
-        finish_kernel,
-        (shape((rows, channels), BF16), shape((blocks, 1, 12 * rows), F32)),
-        n=5,
         name="finish",
-    )(updates, single, out_gain, w_backbone.T, frames)
+    )(updates, single, out_gain, w_backbone.T)
     middle_first = [(k + blocks // 2) % blocks for k in range(blocks)]
     received = lax.all_to_all(
         send, "blk", split_axis=0, concat_axis=0, axis_index_groups=[middle_first], tiled=True
     )
-    frames_out = call(
+    frames_out, single_out = call(
         functools.partial(spread_kernel, middle_first[0]),
-        shape((12, blocks * rows), F32),
-        n=1,
+        (shape((12, blocks * rows), F32), shape((rows, channels), BF16)),
+        (pltpu.VMEM((8, blocks * rows), F32),),
+        n=3,
         name="spread",
-    )(received)
+    )(received, all_frames, single_here)
     return (single_out, frames_out)
 
 

time: 130 us -> 128 us (0.985)
  no operation moved by 1% of the time
where the time goes in v5:
time: 128 us; the launch traced here: 127 us
  blocking collectives  110 us (86%)
  Pallas kernels  9.36 us (7%)
  starting transfers between devices  5.57 us (4%)
  waiting for transfers between devices  1.68 us (1%)
    all_gather x1, blocking collectives, body(): lax.all_gather(payload, 'blk', axis=0, axis_index_groups=ways, tiled=False)  74.3 us
    all_to_all x1, blocking collectives, body(): lax.all_to_all(send, 'blk', split_axis=0, concat_axis=0, axis_index_group...  25.4 us
    all_to_all x1, blocking collectives, body(): lax.all_to_all(updates, 'head', split_axis=0, concat_axis=0, axis_index_g...  10.1 us
    ppermute x1, starting transfers between devices, body(): across = lax.ppermute(gathered, 'blk', swap)  3.61 us
    pallas_call x1, Pallas kernels, body(): call(functools.partial(near_kernel, heads, n_query), (shape((HALF, 3 * HA...  2.85 us
  transfers between devices with their start and end apart: 2, of which 2 were waited for; matrix products, arithmetic and copies ran while one was open for 0% of the time, Pallas kernels for 3%

profile of v5, /device:TPU:40, one launch (start us, length us, event | category | flops | bytes accessed | tf_op | source)
XLA Modules:
  0.0 127.3 jit_solution(3759219571583814600)
XLA Ops:
  0.6 0.0 copy-start.2
  0.6 0.0 copy-start.5
  0.7 0.0 copy-start.6
  0.7 0.0 copy-start.7
  0.7 0.0 copy-start.8
  0.7 0.0 copy-start.9
  0.7 0.0 copy-start.10
  0.7 0.0 copy-start.11
  0.7 0.0 copy-start
  0.7 1.5 %keys.1 = f32[16,256]{1,0:T(8,128)S(1)} custom-call(bf16[32,384]{1,0:T(8,128)(2,1)} %single_ref.3, f32[12,32]{1,0:T(8,128)} %frames_ref.1, s32[32]{0:T(128)} %chain_ref.1, s32[32]{0:T(128)} %mask_ref.1, bf16[96,384]{1,0:T(8,128)(2,1)} %bitcast.18, bf16[108,384]{1,0:T(8,128)(2,1)} %bitcast.17), custom_call_target="tpu_custom_call" | custom-call | flops 10000000000 | bytes 8388608 | tf_op jit(solution)/shard_map/keys/pallas_call | solution.py:491
  2.2 74.3 %all-gather = f32[256,256]{1,0:T(8,128)S(1)} all-gather(f32[16,256]{1,0:T(8,128)S(1)} %keys.1), channel_id=2, replica_groups={{0,16,32,48,64,80,96,112,128,144,160,176,192,208,224,240},{8,24,40,56,7..., dimensions={0}, use_global_device_ids=true | all-gather | bytes 278528 | tf_op jit(solution)/shard_map/all_gather | solution.py:507
  76.5 3.6 %collective-permute-start = (f32[16,16,256]{2,1,0:T(8,128)S(1)}, f32[16,16,256]{2,1,0:T(8,128)S(1)}, u32[]{:S(2)}, u32[]{:S(2)}) collective-permute-start(f32[16,16,256]{2,1,0:T(8,128)S(1)} %bitcast.10), channel_id=1, source_target_pairs={{0,8},{8,0},{16,24},{24,16},{32,40},{40,32},{48,56},{56,48},{64,72... | collective-permute-start | bytes 786440 | tf_op jit(solution)/shard_map/ppermute | solution.py:509
  80.1 0.0 copy-done.2
  80.1 0.0 copy-done.5
  80.1 0.0 copy-done.6
  80.1 0.0 copy-done.7
  80.2 0.0 copy-done.8
  80.2 0.0 copy-done.9
  80.2 0.0 copy-done.10
  80.2 0.0 copy-done.11
  80.2 1.0 queries.1
  81.2 0.0 copy-done
  81.2 0.0 copy-start.1
  81.3 2.9 %near.1 = (f32[128,384]{1,0:T(8,128)S(1)}, f32[256,128]{1,0:T(8,128)S(1)}) custom-call(bf16[32,16,2,16,128]{4,3,2,1,0:T(8,128)(2,1)S(1)} %bitcast.8, bf16[3,128]{1,0:T(4,128)(2,1)} %bitcast.16, f32[16,16,256]{2,1,0:T(8,128)S(1)} %bitcast.11, f32[128,128]{1,0:T(8,128)S(1)} %get-tuple-element.11.qb_ref, f32[16,128]{1,0:T(8,128)S(1)} %get-tuple-element.12.qaux_ref), custom_call_target="tpu_custom_call" | custom-call | flops 1000000000 | bytes 4194304 | tf_op jit(solution)/shard_map/near/pallas_call | solution.py:523
  84.1 0.0 copy-start.3
  84.1 0.0 copy-start.4
  84.1 0.6 collective-permute-done.across_ref
  84.8 1.4 %across.1.mine_ref = f32[128,384]{1,0:T(8,128)S(1)} custom-call(f32[128,384]{1,0:T(8,128)S(1)} %get-tuple-element.13.part_in, f32[16,16,256]{2,1,0:T(8,128)S(1)} %collective-permute-done.across_ref, f32[256,128]{1,0:T(8,128)S(1)} %get-tuple-element.14.bias_ref, f32[128,128]{1,0:T(8,128)S(1)} %get-tuple-element.11.qb_ref, ...), custom_call_target="tpu_custom_call" | custom-call | tf_op jit(solution)/shard_map/across/pallas_call | solution.py:537
  86.1 2.0 %collective-permute-start.1 = (f32[128,384]{1,0:T(8,128)S(1)}, f32[128,384]{1,0:T(8,128)S(1)}, u32[]{:S(2)}, u32[]{:S(2)}) collective-permute-start(f32[128,384]{1,0:T(8,128)S(1)} %across.1.mine_ref), channel_id=1, source_target_pairs={{0,1},{1,0},{2,3},{3,2},{4,5},{5,4},{6,7},{7,6},{8,9},{9,8},{10,11... | collective-permute-start | bytes 589832 | tf_op jit(solution)/shard_map/ppermute | solution.py:545
  88.1 0.4 frames.1._.frames_ref
  88.5 1.0 collective-permute-done.1.theirs_ref
  89.5 0.0 copy-done.1
  89.5 1.1 merge.1
  90.6 10.1 %all_to_all.10.updates_ref = f32[4,32,384]{2,1,0:T(8,128)S(1)} all-to-all(f32[4,32,384]{2,1,0:T(8,128)S(1)} %merge.1), channel_id=1, replica_groups={{6,0,2,4},{7,1,3,5},{14,8,10,12},{15,9,11,13},{22,16,18,20},{23,17,19,2..., dimensions={0} | all-to-all | bytes 393216 | tf_op jit(solution)/shard_map/all_to_all | solution.py:563
  100.7 0.0 copy-done.3
  100.7 0.0 copy-done.4
  100.7 0.5 finish.1
  101.1 25.4 %all_to_all.11.blocks_ref = f32[32,1,256]{2,1,0:T(1,128)S(1)} all-to-all(f32[32,1,256]{2,1,0:T(1,128)S(1)} %get-tuple-element.16), channel_id=1, replica_groups={{128,136,144,152,160,168,176,184,192,200,208,216,224,232,240,248,0,8,16..., dimensions={0} | all-to-all | bytes 65536 | tf_op jit(solution)/shard_map/all_to_all | solution.py:573
  126.5 0.8 spread.1
Async XLA Ops:
  0.6 79.5 %copy-start.2 = (bf16[32,384]{1,0:T(8,128)(2,1)S(1)}, bf16[32,384]{1,0:T(8,128)(2,1)}, u32[]{:S(2)}) copy-start(bf16[32,384]{1,0:T(8,128)(2,1)} %single_ref.3) | copy-start | bytes 73732
  0.6 79.5 %copy-start.5 = (bf16[384,48]{0,1:T(8,128)(2,1)S(1)}, bf16[384,48]{0,1:T(8,128)(2,1)}, u32[]{:S(2)}) copy-start(bf16[384,48]{0,1:T(8,128)(2,1)} %param.20) | copy-start | bytes 110596
  0.7 79.5 %copy-start.6 = (bf16[384,36]{0,1:T(8,128)(2,1)S(1)}, bf16[384,36]{0,1:T(8,128)(2,1)}, u32[]{:S(2)}) copy-start(bf16[384,36]{0,1:T(8,128)(2,1)} %param.22) | copy-start | bytes 82948
  0.7 79.5 %copy-start.7 = (f32[12,32]{1,0:T(8,128)S(1)}, f32[12,32]{1,0:T(8,128)}, u32[]{:S(2)}) copy-start(f32[12,32]{1,0:T(8,128)} %frames_ref.1) | copy-start | bytes 4612
  0.7 79.5 %copy-start.8 = (s32[32]{0:T(128)S(1)}, s32[32]{0:T(128)}, u32[]{:S(2)}) copy-start(s32[32]{0:T(128)} %chain_ref.1) | copy-start | bytes 388
  0.7 79.5 %copy-start.9 = (s32[32]{0:T(128)S(1)}, s32[32]{0:T(128)}, u32[]{:S(2)}) copy-start(s32[32]{0:T(128)} %mask_ref.1) | copy-start | bytes 388
  0.7 79.5 %copy-start.10 = (f32[3]{0:T(128)S(1)}, f32[3]{0:T(128)}, u32[]{:S(2)}) copy-start(f32[3]{0:T(128)} %hw_ref.1) | copy-start | bytes 40
  0.7 79.5 %copy-start.11 = (f32[3]{0:T(128)S(1)}, f32[3]{0:T(128)}, u32[]{:S(2)}) copy-start(f32[3]{0:T(128)} %cb_ref.1) | copy-start | bytes 40
  0.7 80.5 %copy-start = (bf16[32,32,16,128]{3,2,1,0:T(8,128)(2,1)S(1)}, bf16[32,32,16,128]{3,2,1,0:T(8,128)(2,1)}, u32[]{:S(2)}) copy-start(bf16[32,32,16,128]{3,2,1,0:T(8,128)(2,1)} %param.16) | copy-start | bytes 12582916
  76.5 8.3 %collective-permute-start = (f32[16,16,256]{2,1,0:T(8,128)S(1)}, f32[16,16,256]{2,1,0:T(8,128)S(1)}, u32[]{:S(2)}, u32[]{:S(2)}) collective-permute-start(f32[16,16,256]{2,1,0:T(8,128)S(1)} %bitcast.10), channel_id=1, source_target_pairs={{0,8},{8,0},{16,24},{24,16},{32,40},{40,32},{48,56},{56,48},{64,72... | collective-permute-start | bytes 786440 | tf_op jit(solution)/shard_map/ppermute | solution.py:509
  81.2 8.3 %copy-start.1 = (bf16[3,176,384]{2,1,0:T(8,128)(2,1)S(1)}, bf16[3,176,384]{2,1,0:T(8,128)(2,1)}, u32[]{:S(2)}) copy-start(bf16[3,176,384]{2,1,0:T(8,128)(2,1)} %w_out_ref.1) | copy-start | bytes 1216516
  84.1 16.5 %copy-start.3 = (bf16[384,6]{0,1:T(8,128)(2,1)S(1)}, bf16[384,6]{0,1:T(8,128)(2,1)}, u32[]{:S(2)}) copy-start(bf16[384,6]{0,1:T(8,128)(2,1)} %param.29) | copy-start | bytes 13828
  84.1 16.5 %copy-start.4 = (f32[384]{0:T(512)S(1)}, f32[384]{0:T(512)}, u32[]{:S(2)}) copy-start(f32[384]{0:T(512)} %gain_ref.1) | copy-start | bytes 4612
  86.1 3.4 %collective-permute-start.1 = (f32[128,384]{1,0:T(8,128)S(1)}, f32[128,384]{1,0:T(8,128)S(1)}, u32[]{:S(2)}, u32[]{:S(2)}) collective-permute-start(f32[128,384]{1,0:T(8,128)S(1)} %across.1.mine_ref), channel_id=1, source_target_pairs={{0,1},{1,0},{2,3},{3,2},{4,5},{5,4},{6,7},{7,6},{8,9},{9,8},{10,11... | collective-permute-start | bytes 589832 | tf_op jit(solution)/shard_map/ppermute | solution.py:545

commit v6 on v5

--- a/solution.py
+++ b/solution.py
@@ -200,6 +200,10 @@
     return top, dot(weights, block, HIGH)
 
 
+def ascending(ref):
+    return jnp.concatenate([ref[k] for k in reversed(range(ref.shape[0]))], axis=0)
+
+
 def side(pair_ref, i, parity):
     _, far, _, half, width = pair_ref.shape
     return pair_ref[i, :, parity].reshape(far * half, width)
@@ -236,7 +240,7 @@
     place = lax.axis_index("blk") % 2
     small = pltpu.make_async_copy(wb_hbm, wb_ref, sem)
     small.start()
-    block = mine_ref[...].reshape(keys, mine_ref.shape[2])
+    block = ascending(mine_ref)
     partial, penalty = scores(n_query, block, qb_ref, qaux_ref)
     lane = iota((width, HALF), 1)
     row = iota((HALF, width), 0)
@@ -267,10 +271,9 @@
 def across_kernel(
     n_query, part_in, across_ref, bias_ref, qb_ref, qaux_ref, pair_ref, part_ref, turned_w
 ):
-    far, half, lanes = across_ref.shape
     width = pair_ref.shape[4]
     place = lax.axis_index("blk") % 2
-    block = across_ref[...].reshape(far * half, lanes)
+    block = ascending(across_ref)
     partial, penalty = scores(n_query, block, qb_ref, qaux_ref)
     logits = (partial + LOGIT_WEIGHT * bias_ref[...]) - penalty
     top, sums = softmax_sums(logits, block, turned_w)
@@ -394,7 +397,7 @@
         own = pltpu.roll(x, HALF - edge, 1)
         other = pltpu.roll(x, HALF - edge - 12, 1)
         for k in range(far):
-            base = (2 * k + parity) * 2 * half
+            base = (2 * (far - 1 - k) + parity) * 2 * half
             rows = slice(k * half, (k + 1) * half)
             order[pl.ds(pl.multiple_of(base + which * half, half), half), :] = own[rows, :]
             order[pl.ds(pl.multiple_of(base + (1 - which) * half, half), half), :] = other[rows, :]
@@ -503,7 +506,7 @@
         cost=pl.CostEstimate(flops=10**10, bytes_accessed=4 * pair.size, transcendentals=0),
         name="keys",
     )(*(in_hbm(x) for x in inputs))
-    ways = [list(range(k, blocks, 2)) for k in range(2)]
+    ways = [list(range(k, blocks, 2))[::-1] for k in range(2)]
     gathered = lax.all_gather(payload, "blk", axis=0, axis_index_groups=ways, tiled=False)
     swap = [(k, k + 1 - 2 * (k % 2)) for k in range(blocks)]
     across = lax.ppermute(gathered, "blk", swap)

time: 128 us -> 126 us (0.984)
  no operation moved by 1% of the time
where the time goes in v6:
time: 126 us
  blocking collectives  109 us (87%)
  Pallas kernels  9.35 us (7%)
  starting transfers between devices  5.44 us (4%)
  waiting for transfers between devices  1.81 us (1%)
    all_gather x1, blocking collectives, body(): lax.all_gather(payload, 'blk', axis=0, axis_index_groups=ways, tiled=False)  73.2 us
    all_to_all x1, blocking collectives, body(): lax.all_to_all(send, 'blk', split_axis=0, concat_axis=0, axis_index_group...  25.5 us
    all_to_all x1, blocking collectives, body(): lax.all_to_all(updates, 'head', split_axis=0, concat_axis=0, axis_index_g...  9.89 us
    ppermute x1, starting transfers between devices, body(): across = lax.ppermute(gathered, 'blk', swap)  3.48 us
    pallas_call x1, Pallas kernels, body(): call(functools.partial(near_kernel, heads, n_query), (shape((HALF, 3 * HA...  2.85 us
  transfers between devices with their start and end apart: 2, of which 2 were waited for; matrix products, arithmetic and copies ran while one was open for 0% of the time, Pallas kernels for 3%

profile of v6, /device:TPU:40, one launch (start us, length us, event | category | flops | bytes accessed | tf_op | source)
XLA Modules:
  0.0 126.1 jit_solution(4469897616854709708)
XLA Ops:
  0.6 0.0 copy-start.2
  0.6 0.0 copy-start.5
  0.7 0.0 copy-start.6
  0.7 0.0 copy-start.7
  0.7 0.0 copy-start.8
  0.7 0.0 copy-start.9
  0.7 0.0 copy-start.10
  0.7 0.0 copy-start.11
  0.7 0.0 copy-start
  0.7 1.5 %keys.1 = f32[16,256]{1,0:T(8,128)S(1)} custom-call(bf16[32,384]{1,0:T(8,128)(2,1)} %single_ref.3, f32[12,32]{1,0:T(8,128)} %frames_ref.1, s32[32]{0:T(128)} %chain_ref.1, s32[32]{0:T(128)} %mask_ref.1, bf16[96,384]{1,0:T(8,128)(2,1)} %bitcast.18, bf16[108,384]{1,0:T(8,128)(2,1)} %bitcast.17), custom_call_target="tpu_custom_call" | custom-call | flops 10000000000 | bytes 8388608 | tf_op jit(solution)/shard_map/keys/pallas_call | solution.py:494
  2.2 73.2 %all-gather = f32[256,256]{1,0:T(8,128)S(1)} all-gather(f32[16,256]{1,0:T(8,128)S(1)} %keys.1), channel_id=2, replica_groups={{240,224,208,192,176,160,144,128,112,96,80,64,48,32,16,0},{248,232,216,..., dimensions={0}, use_global_device_ids=true | all-gather | bytes 278528 | tf_op jit(solution)/shard_map/all_gather | solution.py:510
  75.4 3.5 %collective-permute-start = (f32[16,16,256]{2,1,0:T(8,128)S(1)}, f32[16,16,256]{2,1,0:T(8,128)S(1)}, u32[]{:S(2)}, u32[]{:S(2)}) collective-permute-start(f32[16,16,256]{2,1,0:T(8,128)S(1)} %bitcast.10), channel_id=1, source_target_pairs={{0,8},{8,0},{16,24},{24,16},{32,40},{40,32},{48,56},{56,48},{64,72... | collective-permute-start | bytes 786440 | tf_op jit(solution)/shard_map/ppermute | solution.py:512
  78.9 0.0 copy-done.2
  78.9 0.0 copy-done.5
  78.9 0.0 copy-done.6
  78.9 0.0 copy-done.7
  78.9 0.0 copy-done.8
  79.0 0.0 copy-done.9
  79.0 0.0 copy-done.10
  79.0 0.0 copy-done.11
  79.0 1.0 queries.1
  80.0 0.0 copy-done
  80.0 0.0 copy-start.1
  80.0 2.9 %near.1 = (f32[128,384]{1,0:T(8,128)S(1)}, f32[256,128]{1,0:T(8,128)S(1)}) custom-call(bf16[32,16,2,16,128]{4,3,2,1,0:T(8,128)(2,1)S(1)} %bitcast.8, bf16[3,128]{1,0:T(4,128)(2,1)} %bitcast.16, f32[16,16,256]{2,1,0:T(8,128)S(1)} %bitcast.11, f32[128,128]{1,0:T(8,128)S(1)} %get-tuple-element.11.qb_ref, f32[16,128]{1,0:T(8,128)S(1)} %get-tuple-element.12.qaux_ref), custom_call_target="tpu_custom_call" | custom-call | flops 1000000000 | bytes 4194304 | tf_op jit(solution)/shard_map/near/pallas_call | solution.py:526
  82.9 0.0 copy-start.3
  82.9 0.0 copy-start.4
  82.9 0.8 collective-permute-done.across_ref
  83.7 1.3 %across.1.mine_ref = f32[128,384]{1,0:T(8,128)S(1)} custom-call(f32[128,384]{1,0:T(8,128)S(1)} %get-tuple-element.13.part_in, f32[16,16,256]{2,1,0:T(8,128)S(1)} %collective-permute-done.across_ref, f32[256,128]{1,0:T(8,128)S(1)} %get-tuple-element.14.bias_ref, f32[128,128]{1,0:T(8,128)S(1)} %get-tuple-element.11.qb_ref, ...), custom_call_target="tpu_custom_call" | custom-call | tf_op jit(solution)/shard_map/across/pallas_call | solution.py:540
  85.0 2.0 %collective-permute-start.1 = (f32[128,384]{1,0:T(8,128)S(1)}, f32[128,384]{1,0:T(8,128)S(1)}, u32[]{:S(2)}, u32[]{:S(2)}) collective-permute-start(f32[128,384]{1,0:T(8,128)S(1)} %across.1.mine_ref), channel_id=1, source_target_pairs={{0,1},{1,0},{2,3},{3,2},{4,5},{5,4},{6,7},{7,6},{8,9},{9,8},{10,11... | collective-permute-start | bytes 589832 | tf_op jit(solution)/shard_map/ppermute | solution.py:548
  87.0 0.4 frames.1._.frames_ref
  87.4 1.0 collective-permute-done.1.theirs_ref
  88.4 0.0 copy-done.1
  88.4 1.1 merge.1
  89.5 9.9 %all_to_all.10.updates_ref = f32[4,32,384]{2,1,0:T(8,128)S(1)} all-to-all(f32[4,32,384]{2,1,0:T(8,128)S(1)} %merge.1), channel_id=1, replica_groups={{6,0,2,4},{7,1,3,5},{14,8,10,12},{15,9,11,13},{22,16,18,20},{23,17,19,2..., dimensions={0} | all-to-all | bytes 393216 | tf_op jit(solution)/shard_map/all_to_all | solution.py:566
  99.4 0.0 copy-done.3
  99.4 0.0 copy-done.4
  99.4 0.5 finish.1
  99.9 25.5 %all_to_all.11.blocks_ref = f32[32,1,256]{2,1,0:T(1,128)S(1)} all-to-all(f32[32,1,256]{2,1,0:T(1,128)S(1)} %get-tuple-element.16), channel_id=1, replica_groups={{128,136,144,152,160,168,176,184,192,200,208,216,224,232,240,248,0,8,16..., dimensions={0} | all-to-all | bytes 65536 | tf_op jit(solution)/shard_map/all_to_all | solution.py:576
  125.3 0.8 spread.1
Async XLA Ops:
  0.6 78.3 %copy-start.2 = (bf16[32,384]{1,0:T(8,128)(2,1)S(1)}, bf16[32,384]{1,0:T(8,128)(2,1)}, u32[]{:S(2)}) copy-start(bf16[32,384]{1,0:T(8,128)(2,1)} %single_ref.3) | copy-start | bytes 73732
  0.6 78.3 %copy-start.5 = (bf16[384,48]{0,1:T(8,128)(2,1)S(1)}, bf16[384,48]{0,1:T(8,128)(2,1)}, u32[]{:S(2)}) copy-start(bf16[384,48]{0,1:T(8,128)(2,1)} %param.20) | copy-start | bytes 110596
  0.7 78.3 %copy-start.6 = (bf16[384,36]{0,1:T(8,128)(2,1)S(1)}, bf16[384,36]{0,1:T(8,128)(2,1)}, u32[]{:S(2)}) copy-start(bf16[384,36]{0,1:T(8,128)(2,1)} %param.22) | copy-start | bytes 82948
  0.7 78.3 %copy-start.7 = (f32[12,32]{1,0:T(8,128)S(1)}, f32[12,32]{1,0:T(8,128)}, u32[]{:S(2)}) copy-start(f32[12,32]{1,0:T(8,128)} %frames_ref.1) | copy-start | bytes 4612
  0.7 78.3 %copy-start.8 = (s32[32]{0:T(128)S(1)}, s32[32]{0:T(128)}, u32[]{:S(2)}) copy-start(s32[32]{0:T(128)} %chain_ref.1) | copy-start | bytes 388
  0.7 78.3 %copy-start.9 = (s32[32]{0:T(128)S(1)}, s32[32]{0:T(128)}, u32[]{:S(2)}) copy-start(s32[32]{0:T(128)} %mask_ref.1) | copy-start | bytes 388
  0.7 78.3 %copy-start.10 = (f32[3]{0:T(128)S(1)}, f32[3]{0:T(128)}, u32[]{:S(2)}) copy-start(f32[3]{0:T(128)} %hw_ref.1) | copy-start | bytes 40
  0.7 78.3 %copy-start.11 = (f32[3]{0:T(128)S(1)}, f32[3]{0:T(128)}, u32[]{:S(2)}) copy-start(f32[3]{0:T(128)} %cb_ref.1) | copy-start | bytes 40
  0.7 79.3 %copy-start = (bf16[32,32,16,128]{3,2,1,0:T(8,128)(2,1)S(1)}, bf16[32,32,16,128]{3,2,1,0:T(8,128)(2,1)}, u32[]{:S(2)}) copy-start(bf16[32,32,16,128]{3,2,1,0:T(8,128)(2,1)} %param.16) | copy-start | bytes 12582916
  75.4 8.3 %collective-permute-start = (f32[16,16,256]{2,1,0:T(8,128)S(1)}, f32[16,16,256]{2,1,0:T(8,128)S(1)}, u32[]{:S(2)}, u32[]{:S(2)}) collective-permute-start(f32[16,16,256]{2,1,0:T(8,128)S(1)} %bitcast.10), channel_id=1, source_target_pairs={{0,8},{8,0},{16,24},{24,16},{32,40},{40,32},{48,56},{56,48},{64,72... | collective-permute-start | bytes 786440 | tf_op jit(solution)/shard_map/ppermute | solution.py:512
  80.0 8.4 %copy-start.1 = (bf16[3,176,384]{2,1,0:T(8,128)(2,1)S(1)}, bf16[3,176,384]{2,1,0:T(8,128)(2,1)}, u32[]{:S(2)}) copy-start(bf16[3,176,384]{2,1,0:T(8,128)(2,1)} %w_out_ref.1) | copy-start | bytes 1216516
  82.9 16.5 %copy-start.3 = (bf16[384,6]{0,1:T(8,128)(2,1)S(1)}, bf16[384,6]{0,1:T(8,128)(2,1)}, u32[]{:S(2)}) copy-start(bf16[384,6]{0,1:T(8,128)(2,1)} %param.29) | copy-start | bytes 13828
  82.9 16.5 %copy-start.4 = (f32[384]{0:T(512)S(1)}, f32[384]{0:T(512)}, u32[]{:S(2)}) copy-start(f32[384]{0:T(512)} %gain_ref.1) | copy-start | bytes 4612
  85.0 3.4 %collective-permute-start.1 = (f32[128,384]{1,0:T(8,128)S(1)}, f32[128,384]{1,0:T(8,128)S(1)}, u32[]{:S(2)}, u32[]{:S(2)}) collective-permute-start(f32[128,384]{1,0:T(8,128)S(1)} %across.1.mine_ref), channel_id=1, source_target_pairs={{0,1},{1,0},{2,3},{3,2},{4,5},{5,4},{6,7},{7,6},{8,9},{9,8},{10,11... | collective-permute-start | bytes 589832 | tf_op jit(solution)/shard_map/ppermute | solution.py:548

commit v7 on v6

--- a/solution.py
+++ b/solution.py
@@ -406,7 +406,7 @@
         out_ref[:, at] = order[at, :].T[0:12, :]
 
 
-def spread_kernel(first, blocks_ref, frames_ref, single_ref, out_ref, single_out_ref, motion):
+def spread_kernel(quads, blocks_ref, frames_ref, single_ref, out_ref, single_out_ref, motion):
     single_out_ref[...] = single_ref[...]
     blocks, _, wide = blocks_ref.shape
     rows = frames_ref.shape[1] // blocks
@@ -424,7 +424,7 @@
             z = jnp.where(g - s == d, up, z)
             z = jnp.where(g - s == d - groups, down, z)
         for q in range(blocks // groups):
-            at = (HALF * q + rows * first) % (rows * blocks)
+            at = HALF * quads[q]
             motion[groups * v : groups * (v + 1), at : at + HALF] = z[
                 groups * q : groups * (q + 1), :
             ]
@@ -572,12 +572,16 @@
         n=4,
         name="finish",
     )(updates, single, out_gain, w_backbone.T)
-    middle_first = [(k + blocks // 2) % blocks for k in range(blocks)]
+    per = HALF // rows
+    count = blocks // per
+    outward = [(count + k // 2 if k % 2 == 0 else count - 1 - k // 2) % count for k in range(count)]
+    quads = [count // 2] + [q for q in outward if q != count // 2]
+    order = [per * q + k for q in quads for k in range(per)]
     received = lax.all_to_all(
-        send, "blk", split_axis=0, concat_axis=0, axis_index_groups=[middle_first], tiled=True
+        send, "blk", split_axis=0, concat_axis=0, axis_index_groups=[order], tiled=True
     )
     frames_out, single_out = call(
-        functools.partial(spread_kernel, middle_first[0]),
+        functools.partial(spread_kernel, quads),
         (shape((12, blocks * rows), F32), shape((rows, channels), BF16)),
         (pltpu.VMEM((8, blocks * rows), F32),),
         n=3,

time: 126 us -> 126 us (level)
  no operation moved by 1% of the time
where the time goes in v7:
time: 126 us
  blocking collectives  108 us (86%)
  Pallas kernels  9.35 us (7%)
  starting transfers between devices  5.44 us (4%)
  waiting for transfers between devices  1.81 us (1%)
    all_gather x1, blocking collectives, body(): lax.all_gather(payload, 'blk', axis=0, axis_index_groups=ways, tiled=False)  73.2 us
    all_to_all x1, blocking collectives, body(): lax.all_to_all(send, 'blk', split_axis=0, concat_axis=0, axis_index_group...  25.4 us
    all_to_all x1, blocking collectives, body(): lax.all_to_all(updates, 'head', split_axis=0, concat_axis=0, axis_index_g...  9.89 us
    ppermute x1, starting transfers between devices, body(): across = lax.ppermute(gathered, 'blk', swap)  3.48 us
    pallas_call x1, Pallas kernels, body(): call(functools.partial(near_kernel, heads, n_query), (shape((HALF, 3 * HA...  2.85 us
  transfers between devices with their start and end apart: 2, of which 2 were waited for; matrix products, arithmetic and copies ran while one was open for 0% of the time, Pallas kernels for 3%

profile of v7, /device:TPU:40, one launch (start us, length us, event | category | flops | bytes accessed | tf_op | source)
XLA Modules:
  0.0 126.0 jit_solution(8164197668351547404)
XLA Ops:
  0.6 0.0 copy-start.2
  0.6 0.0 copy-start.5
  0.7 0.0 copy-start.6
  0.7 0.0 copy-start.7
  0.7 0.0 copy-start.8
  0.7 0.0 copy-start.9
  0.7 0.0 copy-start.10
  0.7 0.0 copy-start.11
  0.7 0.0 copy-start
  0.7 1.5 %keys.1 = f32[16,256]{1,0:T(8,128)S(1)} custom-call(bf16[32,384]{1,0:T(8,128)(2,1)} %single_ref.3, f32[12,32]{1,0:T(8,128)} %frames_ref.1, s32[32]{0:T(128)} %chain_ref.1, s32[32]{0:T(128)} %mask_ref.1, bf16[96,384]{1,0:T(8,128)(2,1)} %bitcast.18, bf16[108,384]{1,0:T(8,128)(2,1)} %bitcast.17), custom_call_target="tpu_custom_call" | custom-call | flops 10000000000 | bytes 8388608 | tf_op jit(solution)/shard_map/keys/pallas_call | solution.py:494
  2.2 73.2 %all-gather = f32[256,256]{1,0:T(8,128)S(1)} all-gather(f32[16,256]{1,0:T(8,128)S(1)} %keys.1), channel_id=2, replica_groups={{240,224,208,192,176,160,144,128,112,96,80,64,48,32,16,0},{248,232,216,..., dimensions={0}, use_global_device_ids=true | all-gather | bytes 278528 | tf_op jit(solution)/shard_map/all_gather | solution.py:510
  75.4 3.5 %collective-permute-start = (f32[16,16,256]{2,1,0:T(8,128)S(1)}, f32[16,16,256]{2,1,0:T(8,128)S(1)}, u32[]{:S(2)}, u32[]{:S(2)}) collective-permute-start(f32[16,16,256]{2,1,0:T(8,128)S(1)} %bitcast.10), channel_id=1, source_target_pairs={{0,8},{8,0},{16,24},{24,16},{32,40},{40,32},{48,56},{56,48},{64,72... | collective-permute-start | bytes 786440 | tf_op jit(solution)/shard_map/ppermute | solution.py:512
  78.9 0.0 copy-done.2
  78.9 0.0 copy-done.5
  78.9 0.0 copy-done.6
  78.9 0.0 copy-done.7
  78.9 0.0 copy-done.8
  79.0 0.0 copy-done.9
  79.0 0.0 copy-done.10
  79.0 0.0 copy-done.11
  79.0 1.0 queries.1
  80.0 0.0 copy-done
  80.0 0.0 copy-start.1
  80.0 2.9 %near.1 = (f32[128,384]{1,0:T(8,128)S(1)}, f32[256,128]{1,0:T(8,128)S(1)}) custom-call(bf16[32,16,2,16,128]{4,3,2,1,0:T(8,128)(2,1)S(1)} %bitcast.8, bf16[3,128]{1,0:T(4,128)(2,1)} %bitcast.16, f32[16,16,256]{2,1,0:T(8,128)S(1)} %bitcast.11, f32[128,128]{1,0:T(8,128)S(1)} %get-tuple-element.11.qb_ref, f32[16,128]{1,0:T(8,128)S(1)} %get-tuple-element.12.qaux_ref), custom_call_target="tpu_custom_call" | custom-call | flops 1000000000 | bytes 4194304 | tf_op jit(solution)/shard_map/near/pallas_call | solution.py:526
  82.9 0.0 copy-start.3
  82.9 0.0 copy-start.4
  82.9 0.8 collective-permute-done.across_ref
  83.7 1.3 %across.1.mine_ref = f32[128,384]{1,0:T(8,128)S(1)} custom-call(f32[128,384]{1,0:T(8,128)S(1)} %get-tuple-element.13.part_in, f32[16,16,256]{2,1,0:T(8,128)S(1)} %collective-permute-done.across_ref, f32[256,128]{1,0:T(8,128)S(1)} %get-tuple-element.14.bias_ref, f32[128,128]{1,0:T(8,128)S(1)} %get-tuple-element.11.qb_ref, ...), custom_call_target="tpu_custom_call" | custom-call | tf_op jit(solution)/shard_map/across/pallas_call | solution.py:540
  85.0 2.0 %collective-permute-start.1 = (f32[128,384]{1,0:T(8,128)S(1)}, f32[128,384]{1,0:T(8,128)S(1)}, u32[]{:S(2)}, u32[]{:S(2)}) collective-permute-start(f32[128,384]{1,0:T(8,128)S(1)} %across.1.mine_ref), channel_id=1, source_target_pairs={{0,1},{1,0},{2,3},{3,2},{4,5},{5,4},{6,7},{7,6},{8,9},{9,8},{10,11... | collective-permute-start | bytes 589832 | tf_op jit(solution)/shard_map/ppermute | solution.py:548
  87.0 0.4 frames.1._.frames_ref
  87.4 1.0 collective-permute-done.1.theirs_ref
  88.4 0.0 copy-done.1
  88.4 1.1 merge.1
  89.5 9.9 %all_to_all.10.updates_ref = f32[4,32,384]{2,1,0:T(8,128)S(1)} all-to-all(f32[4,32,384]{2,1,0:T(8,128)S(1)} %merge.1), channel_id=1, replica_groups={{6,0,2,4},{7,1,3,5},{14,8,10,12},{15,9,11,13},{22,16,18,20},{23,17,19,2..., dimensions={0} | all-to-all | bytes 393216 | tf_op jit(solution)/shard_map/all_to_all | solution.py:566
  99.4 0.0 copy-done.3
  99.4 0.0 copy-done.4
  99.4 0.5 finish.1
  99.9 25.4 %all_to_all.11.blocks_ref = f32[32,1,256]{2,1,0:T(1,128)S(1)} all-to-all(f32[32,1,256]{2,1,0:T(1,128)S(1)} %get-tuple-element.16), channel_id=1, replica_groups={{128,136,144,152,0,8,16,24,224,232,240,248,32,40,48,56,192,200,208,216,..., dimensions={0} | all-to-all | bytes 65536 | tf_op jit(solution)/shard_map/all_to_all | solution.py:580
  125.2 0.8 spread.1
Async XLA Ops:
  0.6 78.3 %copy-start.2 = (bf16[32,384]{1,0:T(8,128)(2,1)S(1)}, bf16[32,384]{1,0:T(8,128)(2,1)}, u32[]{:S(2)}) copy-start(bf16[32,384]{1,0:T(8,128)(2,1)} %single_ref.3) | copy-start | bytes 73732
  0.6 78.3 %copy-start.5 = (bf16[384,48]{0,1:T(8,128)(2,1)S(1)}, bf16[384,48]{0,1:T(8,128)(2,1)}, u32[]{:S(2)}) copy-start(bf16[384,48]{0,1:T(8,128)(2,1)} %param.20) | copy-start | bytes 110596
  0.7 78.3 %copy-start.6 = (bf16[384,36]{0,1:T(8,128)(2,1)S(1)}, bf16[384,36]{0,1:T(8,128)(2,1)}, u32[]{:S(2)}) copy-start(bf16[384,36]{0,1:T(8,128)(2,1)} %param.22) | copy-start | bytes 82948
  0.7 78.3 %copy-start.7 = (f32[12,32]{1,0:T(8,128)S(1)}, f32[12,32]{1,0:T(8,128)}, u32[]{:S(2)}) copy-start(f32[12,32]{1,0:T(8,128)} %frames_ref.1) | copy-start | bytes 4612
  0.7 78.3 %copy-start.8 = (s32[32]{0:T(128)S(1)}, s32[32]{0:T(128)}, u32[]{:S(2)}) copy-start(s32[32]{0:T(128)} %chain_ref.1) | copy-start | bytes 388
  0.7 78.3 %copy-start.9 = (s32[32]{0:T(128)S(1)}, s32[32]{0:T(128)}, u32[]{:S(2)}) copy-start(s32[32]{0:T(128)} %mask_ref.1) | copy-start | bytes 388
  0.7 78.3 %copy-start.10 = (f32[3]{0:T(128)S(1)}, f32[3]{0:T(128)}, u32[]{:S(2)}) copy-start(f32[3]{0:T(128)} %hw_ref.1) | copy-start | bytes 40
  0.7 78.3 %copy-start.11 = (f32[3]{0:T(128)S(1)}, f32[3]{0:T(128)}, u32[]{:S(2)}) copy-start(f32[3]{0:T(128)} %cb_ref.1) | copy-start | bytes 40
  0.7 79.3 %copy-start = (bf16[32,32,16,128]{3,2,1,0:T(8,128)(2,1)S(1)}, bf16[32,32,16,128]{3,2,1,0:T(8,128)(2,1)}, u32[]{:S(2)}) copy-start(bf16[32,32,16,128]{3,2,1,0:T(8,128)(2,1)} %param.16) | copy-start | bytes 12582916
  75.4 8.3 %collective-permute-start = (f32[16,16,256]{2,1,0:T(8,128)S(1)}, f32[16,16,256]{2,1,0:T(8,128)S(1)}, u32[]{:S(2)}, u32[]{:S(2)}) collective-permute-start(f32[16,16,256]{2,1,0:T(8,128)S(1)} %bitcast.10), channel_id=1, source_target_pairs={{0,8},{8,0},{16,24},{24,16},{32,40},{40,32},{48,56},{56,48},{64,72... | collective-permute-start | bytes 786440 | tf_op jit(solution)/shard_map/ppermute | solution.py:512
  80.0 8.4 %copy-start.1 = (bf16[3,176,384]{2,1,0:T(8,128)(2,1)S(1)}, bf16[3,176,384]{2,1,0:T(8,128)(2,1)}, u32[]{:S(2)}) copy-start(bf16[3,176,384]{2,1,0:T(8,128)(2,1)} %w_out_ref.1) | copy-start | bytes 1216516
  82.9 16.5 %copy-start.3 = (bf16[384,6]{0,1:T(8,128)(2,1)S(1)}, bf16[384,6]{0,1:T(8,128)(2,1)}, u32[]{:S(2)}) copy-start(bf16[384,6]{0,1:T(8,128)(2,1)} %param.29) | copy-start | bytes 13828
  82.9 16.5 %copy-start.4 = (f32[384]{0:T(512)S(1)}, f32[384]{0:T(512)}, u32[]{:S(2)}) copy-start(f32[384]{0:T(512)} %gain_ref.1) | copy-start | bytes 4612
  85.0 3.4 %collective-permute-start.1 = (f32[128,384]{1,0:T(8,128)S(1)}, f32[128,384]{1,0:T(8,128)S(1)}, u32[]{:S(2)}, u32[]{:S(2)}) collective-permute-start(f32[128,384]{1,0:T(8,128)S(1)} %across.1.mine_ref), channel_id=1, source_target_pairs={{0,1},{1,0},{2,3},{3,2},{4,5},{5,4},{6,7},{7,6},{8,9},{9,8},{10,11... | collective-permute-start | bytes 589832 | tf_op jit(solution)/shard_map/ppermute | solution.py:548
